TPU v7x, 32 devices: a whole 2x2x4 slice. The times are simulated.
32 devices in a mesh: seq: 8 (over z, y), tp: 4 (over x, core).
Axes of the slice: x: 2, y: 2, z: 4, core: 2. Of those that a mesh axis runs over, the one named last changes fastest.
Arguments:
- tokens: bfloat16 [8192, 1024], P(('seq', 'tp')), may hold values from -6 to 6
- fine_gain: float32 [1024], replicated, may hold values from 0.1 to 1.9
- fine_query: bfloat16 [1024, 1024], replicated, may hold values from -2.0625 to 2.0625
- fine_keyval: bfloat16 [1024, 2048], replicated, may hold values from -0.125 to 0.125
- fine_out: bfloat16 [1024, 1024], replicated, may hold values from -0.1875 to 0.1875
- down_weight: bfloat16 [1024, 4096], P(None, 'tp'), may hold values from -0.1875 to 0.1875
- coarse_gain: float32 [4096], replicated, may hold values from 0.1 to 1.9
- coarse_query: bfloat16 [4096, 4096], P('seq', 'tp'), may hold values from -1.03125 to 1.03125
- coarse_keyval: bfloat16 [4096, 2, 4096], P('seq', None, 'tp'), may hold values from -0.0625 to 0.0625
- coarse_out: bfloat16 [4096, 4096], P('tp'), may hold values from -0.09375 to 0.09375
- up_weight: bfloat16 [4096, 1024], P('tp'), may hold values from -0.09375 to 0.09375
Outputs:
- result: bfloat16 [8192, 1024], P(('seq', 'tp'))
All inputs are finite; a program needn't handle non-finite values.
Results may differ from a plain program's by a relative error of at most 0.02.
Values may be sent and summed in bfloat16 or wider, within the bound.
A program may use at most 192 MiB of HBM per device.

v0:
```python
import functools
import math

import jax
import jax.numpy as jnp
from jax import lax
from jax.experimental import pallas as pl
from jax.experimental.pallas import tpu as pltpu
from jax.sharding import PartitionSpec as P

HEAD = 128
WINDOW = 256
SHORT = 8


epsilon = 1e-06
big_negative = -1e30


def from_behind(array, axis, by):
    size = lax.axis_size(axis)
    pairs = [(i, i + by) for i in range(size) if 0 <= i + by < size]
    return lax.ppermute(array, axis, pairs)


def normalize(values, scale_gain):
    mean_square = jnp.mean(values * values, axis=-1, keepdims=True)
    return values * lax.rsqrt(mean_square + epsilon) * scale_gain


def online_update(state, query_heads, key_piece, value_piece, query_index):
    running_max, running_sum, accumulate = state
    scale = 1.0 / math.sqrt(HEAD)
    scores = (
        jnp.einsum("qhd,khd->hqk", query_heads, key_piece, preferred_element_type=jnp.float32)
        * scale
    )
    key_index = jnp.arange(key_piece.shape[0], dtype=jnp.int32)
    allowed = key_index[None, :] <= query_index[:, None]
    scores = jnp.where(allowed[None], scores, big_negative)
    new_max = jnp.maximum(running_max, jnp.max(scores, axis=-1))
    terms = jnp.where(allowed[None], jnp.exp(scores - new_max[..., None]), 0.0)
    new_sum = jnp.sum(terms, axis=-1)
    product = jnp.einsum(
        "hqk,khd->hqd", terms.astype(jnp.bfloat16), value_piece, preferred_element_type=jnp.float32
    )
    return (new_max, new_sum, product)


def body(
    tokens,
    fine_gain,
    fine_query,
    fine_keyval,
    fine_out,
    down_weight,
    coarse_gain,
    coarse_query,
    coarse_keyval,
    coarse_out,
    up_weight,
):
    tok_rows = tokens.shape[0]
    width = tokens.shape[1]
    fine_heads = width // HEAD
    scale = 1.0 / math.sqrt(HEAD)
    start_row = lax.axis_index(("seq", "tp")) * tok_rows
    inputs = tokens.astype(jnp.float32)
    normed = normalize(inputs, fine_gain).astype(jnp.bfloat16)
    queries = jnp.dot(normed, fine_query, preferred_element_type=jnp.float32).astype(jnp.bfloat16)
    keyvals = jnp.dot(normed, fine_keyval, preferred_element_type=jnp.float32).astype(jnp.bfloat16)
    earlier = from_behind(keyvals, ("seq", "tp"), 1)
    key_rows = jnp.concatenate([earlier, keyvals], 0)
    span = key_rows.shape[0]
    key_heads = key_rows[:, :width].reshape(span, fine_heads, HEAD)
    value_heads = key_rows[:, width:].reshape(span, fine_heads, HEAD)
    query_heads = queries.reshape(tok_rows, fine_heads, HEAD)
    scores = (
        jnp.einsum("qhd,khd->hqk", query_heads, key_heads, preferred_element_type=jnp.float32)
        * scale
    )
    row_index = jnp.arange(tok_rows, dtype=jnp.int32)[:, None]
    col_index = jnp.arange(span, dtype=jnp.int32)[None, :]
    offset = row_index + WINDOW - col_index
    allowed = (offset >= 0) & (offset < WINDOW) & (start_row - WINDOW + col_index >= 0)
    scores = jnp.where(allowed[None], scores, big_negative)
    peak = jnp.max(scores, axis=-1, keepdims=True)
    terms = jnp.where(allowed[None], jnp.exp(scores - peak), 0.0)
    denom = jnp.sum(terms, axis=-1)
    mixed = jnp.einsum(
        "hqk,khd->qhd", terms.astype(jnp.bfloat16), value_heads, preferred_element_type=jnp.float32
    )
    local = (mixed / jnp.transpose(denom)[..., None]).reshape(tok_rows, width).astype(jnp.bfloat16)
    fine_state = (inputs + jnp.dot(local, fine_out, preferred_element_type=jnp.float32)).astype(
        jnp.bfloat16
    )
    pooled = jnp.mean(
        fine_state.astype(jnp.float32).reshape(tok_rows // SHORT, SHORT, width), axis=1
    ).astype(jnp.bfloat16)
    pooled_all = lax.all_gather(pooled, "tp", axis=0, tiled=True)
    short_cols = jnp.dot(pooled_all, down_weight, preferred_element_type=jnp.float32).astype(
        jnp.bfloat16
    )
    shortened = lax.all_gather(short_cols, "tp", axis=1, tiled=True)
    coarse_normed = normalize(shortened.astype(jnp.float32), coarse_gain).astype(jnp.bfloat16)
    coarse_rows = coarse_normed.shape[0]
    local_cols = coarse_query.shape[1]
    local_heads = local_cols // HEAD
    query_rows = lax.all_gather(coarse_query, "seq", axis=0, tiled=True)
    keyval_rows = lax.all_gather(coarse_keyval, "seq", axis=0, tiled=True)
    count = query_rows.shape[0]
    query_sum = jnp.dot(coarse_normed, query_rows, preferred_element_type=jnp.float32)
    keyval_sum = jnp.dot(
        coarse_normed,
        keyval_rows.reshape(count, 2 * local_cols),
        preferred_element_type=jnp.float32,
    )
    coarse_queries = query_sum.astype(jnp.bfloat16).reshape(coarse_rows, local_heads, HEAD)
    coarse_kv = keyval_sum.astype(jnp.bfloat16).reshape(coarse_rows, 2, local_cols)
    my_first = lax.axis_index("seq") * coarse_rows
    query_index = my_first + jnp.arange(coarse_rows, dtype=jnp.int32)
    initial = (
        jnp.full((local_heads, coarse_rows), big_negative, jnp.float32),
        jnp.zeros((local_heads, coarse_rows), jnp.float32),
        jnp.zeros((local_heads, coarse_rows, HEAD), jnp.float32),
    )
    piece = lax.all_gather(coarse_kv, "seq", axis=0, tiled=True)
    count = piece.shape[0]
    key_piece = piece[:, 0].reshape(count, local_heads, HEAD)
    value_piece = piece[:, 1].reshape(count, local_heads, HEAD)
    final = lax.cond(
        jnp.int32(0) < my_first + coarse_rows,
        lambda: online_update(initial, coarse_queries, key_piece, value_piece, query_index),
        lambda: initial,
    )
    head_out = final[2] / final[1][..., None]
    coarse_heads = (
        jnp.transpose(head_out, (1, 0, 2)).reshape(coarse_rows, local_cols).astype(jnp.bfloat16)
    )
    partials = jnp.dot(coarse_heads, coarse_out, preferred_element_type=jnp.float32)
    attended = lax.psum_scatter(
        partials.astype(jnp.bfloat16), "tp", scatter_dimension=1, tiled=True
    ).astype(jnp.float32)
    coarse_state = (short_cols.astype(jnp.float32) + attended).astype(jnp.bfloat16)
    prior_row = from_behind(coarse_state[coarse_rows - 1 :], "seq", 1)
    delayed = jnp.concatenate([prior_row, coarse_state[: coarse_rows - 1]], 0)
    lifted = lax.psum_scatter(
        jnp.dot(delayed, up_weight, preferred_element_type=jnp.float32).astype(jnp.bfloat16),
        "tp",
        scatter_dimension=0,
        tiled=True,
    ).astype(jnp.float32)
    result = fine_state.astype(jnp.float32) + jnp.repeat(lifted, SHORT, axis=0)
    return result.astype(jnp.bfloat16)


def flip(index, bit):
    return index + bit - 2 * bit * lax.rem(lax.div(index, jnp.int32(bit)), jnp.int32(2))


def bits_of(size):
    out, bit = [], size // 2
    while bit:
        out.append(bit)
        bit //= 2
    return out


def dot32(left, right):
    return jnp.dot(left, right, preferred_element_type=jnp.float32)


def dot_t(left, right):
    return lax.dot_general(
        left, right, (((1,), (1,)), ((), ())), preferred_element_type=jnp.float32
    )


def section_kernel(
    seq, tp,
    tokens, fine_gain, fine_query, fine_keyval, fine_out, down_weight, coarse_gain, coarse_query,
    coarse_kv, coarse_out, up_weight,
    result,
    both, wq, wkv, wo, down_all, weights, wout, wup,
    normed, queries, key_rows, local, fine_state, pooled_all, coarse_normed, projected, sums,
    heads_out, heads_in, coarse_heads, short_cols, send1, recv1, state, prior, send2, recv2,
    load_sem, halo_s, halo_r, w_s, w_r, d_s, d_r, p_s, p_r, h_s, h_r, r1_s, r1_r, row_s, row_r,
    r2_s, r2_r,
):
    me_s = lax.axis_index("seq")
    me_t = lax.axis_index("tp")
    rows, width = tokens.shape
    scale = 1.0 / math.sqrt(HEAD)
    total = seq * tp
    lin = me_s * tp + me_t
    after = lax.rem(lin + 1, total)
    before = lax.rem(lin + total - 1, total)

    def around(index, step, size):
        return lax.rem(index + step, size)

    def remote(src, dst, send, recv, device):
        copy = pltpu.make_async_remote_copy(
            src_ref=src, dst_ref=dst, send_sem=send, recv_sem=recv,
            device_id=device, device_id_type=pl.DeviceIdType.MESH,
        )
        copy.start()
        return copy

    def load(src, dst, index):
        copy = pltpu.make_async_copy(src, dst, load_sem.at[index])
        copy.start()
        return copy

    def linear(index):
        return {"seq": lax.div(index, tp), "tp": lax.rem(index, tp)}

    barrier = pltpu.get_barrier_semaphore()
    peers = [{"seq": around(me_s, d, seq)} for d in range(1, seq)]
    peers += [{"tp": around(me_t, d, tp)} for d in range(1, tp)]
    peers += [linear(after), linear(before)]
    in_tokens = load(tokens, both.at[pl.ds(rows, rows)], 0)
    in_wkv = load(fine_keyval, wkv, 1)
    in_wq = load(fine_query, wq, 2)
    in_wo = load(fine_out, wo, 3)
    in_down = load(down_weight, down_all.at[me_t], 4)
    own = coarse_query.shape[1] // seq

    def head_parts(dest):
        cols = pl.ds(pl.multiple_of(dest * own, own), own)
        sources = [coarse_query.at[:, cols], coarse_kv.at[0, :, cols], coarse_kv.at[1, :, cols]]
        return [(part, weights.at[me_s, :, pl.ds(k * own, own)]) for k, part in enumerate(sources)]

    in_w = [load(src, dst, 8 + k) for k, (src, dst) in enumerate(head_parts(me_s))]
    in_wout = load(coarse_out, wout, 6)
    in_wup = load(up_weight, wup, 7)
    for peer in peers:
        pl.semaphore_signal(barrier, inc=1, device_id=peer, device_id_type=pl.DeviceIdType.MESH)
    pl.semaphore_wait(barrier, len(peers))

    halo = remote(tokens, both.at[pl.ds(0, rows)], halo_s, halo_r, linear(after))
    order = sorted(range(1, seq), key=lambda d: abs(2 * d - seq))
    w_copies = {}

    def send_weights(offsets):
        for d in offsets:
            dest = around(me_s, d, seq)
            w_copies[d] = [
                remote(
                    src, dst, w_s.at[3 * (d - 1) + k], w_r.at[3 * (d - 1) + k], {"seq": dest}
                )
                for k, (src, dst) in enumerate(head_parts(dest))
            ]

    early = (seq + 1) // 4
    send_weights(order[:early])
    tp_bits = bits_of(tp)
    gain = fine_gain[...]

    def norm_rows(first):
        values = both[pl.ds(first, rows), :].astype(jnp.float32)
        normed[pl.ds(first, rows), :] = normalize(values, gain).astype(jnp.bfloat16)

    in_tokens.wait()
    norm_rows(rows)
    in_wq.wait()
    tile = 2 * HEAD

    @pl.loop(0, width // tile)
    def _(i):
        cols = pl.ds(pl.multiple_of(i * tile, tile), tile)
        queries[:, cols] = dot32(normed[rows:, :], wq[:, cols]).astype(jnp.bfloat16)

    in_wkv.wait()

    def project_rows(first):
        @pl.loop(0, 2 * width // tile)
        def _(i):
            cols = pl.ds(pl.multiple_of(i * tile, tile), tile)
            key_rows[pl.ds(first, rows), cols] = dot32(
                normed[pl.ds(first, rows), :], wkv[:, cols]
            ).astype(jnp.bfloat16)

    project_rows(rows)
    d_first = [
        remote(
            down_weight, down_all.at[me_t], d_s.at[bit - 1], d_r.at[bit - 1],
            {"tp": flip(me_t, bit)},
        )
        for bit in tp_bits
    ]
    halo.wait()
    norm_rows(0)
    project_rows(0)

    row_index = lax.broadcasted_iota(jnp.int32, (rows, 2 * rows), 0)
    col_index = lax.broadcasted_iota(jnp.int32, (rows, 2 * rows), 1)
    offset = row_index + rows - col_index
    allowed = (offset >= 0) & (offset < WINDOW) & (lin * rows - rows + col_index >= 0)

    def attend(query, key, value, mask):
        scores = jnp.where(mask, dot_t(query, key) * scale, big_negative)
        peak = jnp.max(scores, axis=-1, keepdims=True)
        terms = jnp.where(mask, jnp.exp(scores - peak), 0.0)
        denom = jnp.sum(terms, axis=-1, keepdims=True)
        return (dot32(terms.astype(jnp.bfloat16), value) / denom).astype(jnp.bfloat16)

    @pl.loop(0, width // HEAD)
    def _(h):
        cols = pl.ds(pl.multiple_of(h * HEAD, HEAD), HEAD)
        vcols = pl.ds(pl.multiple_of(width + h * HEAD, HEAD), HEAD)
        local[:, cols] = attend(queries[:, cols], key_rows[:, cols], key_rows[:, vcols], allowed)

    in_wo.wait()
    pool_rows = rows // SHORT

    @pl.loop(0, width // tile)
    def _(i):
        cols = pl.ds(pl.multiple_of(i * tile, tile), tile)
        value = both[rows:, cols].astype(jnp.float32) + dot32(local[...], wo[:, cols])
        value = value.astype(jnp.bfloat16)
        fine_state[:, cols] = value
        mean = jnp.mean(value.astype(jnp.float32).reshape(pool_rows, SHORT, tile), axis=1)
        pooled_all[lin, :, cols] = mean.astype(jnp.bfloat16)

    done = []
    held = [lin]
    count = 0
    for axis, bits in (("seq", bits_of(seq)), ("tp", tp_bits)):
        for bit in bits:
            stride = bit * tp if axis == "seq" else bit
            where = {axis: flip(me_s if axis == "seq" else me_t, bit)}
            copies = []
            for slot in held:
                copies.append(
                    remote(
                        pooled_all.at[slot], pooled_all.at[slot], p_s.at[count], p_r.at[count],
                        where,
                    )
                )
                count += 1
            if axis == "seq" and bit == bits[-1]:
                send_weights(order[early:])
            for copy in copies:
                copy.wait_recv()
            done += copies
            held = held + [flip(slot, stride) for slot in held]
    d_done = list(d_first)
    for copy in d_first[:1]:
        copy.wait_recv()
    have = [tp_bits[0]]
    index = tp - 1
    extra = []
    for k, bit in enumerate(tp_bits[1:]):
        subs = list(have)
        now = []
        for sub in subs:
            slot = me_t
            for other in tp_bits:
                if sub & other:
                    slot = flip(slot, other)
            number = bit + sub - 1
            now.append(
                remote(
                    down_all.at[slot], down_all.at[slot], d_s.at[number], d_r.at[number],
                    {"tp": flip(me_t, bit)},
                )
            )
        d_first[k + 1].wait_recv()
        for copy in now:
            copy.wait_recv()
        extra += now
        have = have + [bit] + [bit + sub for sub in subs]
    in_down.wait()

    per = seq // 2 if seq > 1 else 1
    crows = pool_rows * tp
    block = 2 * crows
    cgain = coarse_gain[...]

    @pl.loop(0, seq // 2)
    def _(i):
        first = pl.multiple_of(i * block, block)
        pooled = pooled_all[pl.ds(i * 2 * tp, 2 * tp)].reshape(block, width)
        total_sq = jnp.zeros((block, 1), jnp.float32)
        fcols = down_all.shape[2]
        half = fcols // 2
        for t in range(tp):
            for u in range(2):
                part = dot32(pooled, down_all[t, :, u * half : (u + 1) * half]).astype(jnp.bfloat16)
                wide = part.astype(jnp.float32)
                total_sq += jnp.sum(wide * wide, axis=-1, keepdims=True)
                base = t * fcols + u * half
                coarse_normed[pl.ds(first, block), base : base + half] = part
        factor = lax.rsqrt(total_sq / (tp * fcols) + epsilon)
        for t in range(2 * tp):
            cols = slice(t * half, (t + 1) * half)
            wide = coarse_normed[pl.ds(first, block), cols].astype(jnp.float32)
            coarse_normed[pl.ds(first, block), cols] = (wide * factor * cgain[:, cols]).astype(
                jnp.bfloat16
            )

    mine = pooled_all[pl.ds(me_s * tp, tp)].reshape(crows, width)
    fcols = down_all.shape[2]
    for u in range(2):
        cols = slice(u * fcols // 2, (u + 1) * fcols // 2)
        short_cols[:, cols] = dot32(mine, down_all[me_t, :, cols])
    depth, three = weights.shape[1:]

    for d in [0] + order:
        for copy in w_copies[d] if d else in_w:
            copy.wait_recv() if d else copy.wait()
        source = around(me_s, seq - d, seq)

        @pl.loop(0, seq // 2)
        def _(i, d=d, source=source):
            at = pl.ds(pl.multiple_of(i * block, block), block)
            cols = pl.ds(pl.multiple_of(source * depth, depth), depth)
            product = dot32(coarse_normed[at, cols], weights[source])
            if d == order[-1]:
                projected[at, :] = (sums[at, :] + product).astype(jnp.bfloat16)
            elif d:
                sums[at, :] += product
            else:
                sums[at, :] = product

    for i in range(seq // 2):
        extent = (i + 1) * block
        r = lax.broadcasted_iota(jnp.int32, (block, extent), 0) + i * block
        c = lax.broadcasted_iota(jnp.int32, (block, extent), 1)
        for h in range(own // HEAD):
            part = slice(h * HEAD, (h + 1) * HEAD)
            kpart = slice(own + h * HEAD, own + (h + 1) * HEAD)
            vpart = slice(2 * own + h * HEAD, 2 * own + (h + 1) * HEAD)
            out = attend(
                projected[i * block : extent, part], projected[:extent, kpart],
                projected[:extent, vpart], c <= r,
            )
            heads_out[2 * i : 2 * i + 2, :, part] = out.reshape(2, crows, HEAD)

    heads_in[me_s] = heads_out[me_s]
    h_copies = []
    for d in order:
        dest = around(me_s, d, seq)
        h_copies.append(
            remote(
                heads_out.at[dest], heads_in.at[me_s], h_s.at[d - 1], h_r.at[d - 1],
                {"seq": dest},
            )
        )
    in_wout.wait()
    in_wup.wait()
    for copy in h_copies:
        copy.wait_recv()
    for j in range(seq):
        coarse_heads[:, j * own : (j + 1) * own] = heads_in[j]

    def partial(t, store):
        @pl.loop(0, fcols // tile)
        def _(i):
            cols = pl.ds(pl.multiple_of(i * tile, tile), tile)
            wcols = pl.ds(pl.multiple_of(t * fcols + i * tile, tile), tile)
            store(cols, dot32(coarse_heads[...], wout[:, wcols]))

    tp_order = sorted(range(1, tp), key=lambda d: abs(2 * d - tp))
    r1 = {}
    low_bits = tp_bits[::-1]
    for k, bit in enumerate(low_bits):
        for sub in range(tp - bit, 0, -2 * bit):
            dest = me_t
            for other in tp_bits:
                if sub & other:
                    dest = flip(dest, other)
            for low in low_bits[:k]:
                r1[sub + low].wait_recv()

            def put(cols, value, sub=sub, k=k):
                for low in low_bits[:k]:
                    value += recv1[sub + low - 1, :, cols].astype(jnp.float32)
                send1[sub - 1, :, cols] = value.astype(jnp.bfloat16)

            partial(dest, put)
            r1[sub] = remote(
                send1.at[sub - 1], recv1.at[sub - 1], r1_s.at[sub - 1], r1_r.at[sub - 1],
                {"tp": flip(me_t, bit)},
            )

    def keep(cols, value):
        short_cols[:, cols] = short_cols[:, cols].astype(jnp.bfloat16).astype(jnp.float32) + value

    partial(me_t, keep)
    for bit in low_bits:
        r1[bit].wait_recv()
    whole = short_cols[...]
    for bit in low_bits:
        whole += recv1[bit - 1].astype(jnp.float32)
    state[...] = whole.astype(jnp.bfloat16)
    slab = prior.shape[0]
    row_copy = remote(
        state.at[pl.ds(crows - slab, slab)], prior, row_s, row_r, {"seq": around(me_s, 1, seq)}
    )
    rolled = pltpu.roll(state[...].astype(jnp.float32), 1, 0)
    row_copy.wait_recv()
    previous = prior[...].astype(jnp.float32)[slab - 1 : slab, :]
    previous = jnp.where(me_s > 0, previous, 0.0)
    top = lax.broadcasted_iota(jnp.int32, rolled.shape, 0) == 0
    delayed = jnp.where(top, previous, rolled).astype(jnp.bfloat16)
    coarse_heads[...] = delayed

    @pl.loop(0, width // tile)
    def _(i):
        cols = pl.ds(pl.multiple_of(i * tile, tile), tile)
        short_cols[:, cols] = dot32(coarse_heads[...], wup[:, cols])

    r2 = []
    for d in tp_order:
        dest = around(me_t, d, tp)
        part = short_cols[pl.ds(pl.multiple_of(dest * pool_rows, pool_rows), pool_rows), :]
        send2[d - 1] = part.astype(jnp.bfloat16)
        r2.append(
            remote(
                send2.at[d - 1], recv2.at[d - 1], r2_s.at[d - 1], r2_r.at[d - 1], {"tp": dest}
            )
        )
    lifted = short_cols[pl.ds(pl.multiple_of(me_t * pool_rows, pool_rows), pool_rows), :]
    for copy in r2:
        copy.wait_recv()
    for d in range(1, tp):
        lifted += recv2[d - 1].astype(jnp.float32)
    spread = jnp.broadcast_to(lifted[:, None, :], (pool_rows, SHORT, width)).reshape(rows, width)
    result[...] = (fine_state[...].astype(jnp.float32) + spread).astype(jnp.bfloat16)
    w_flat = [copy for group in w_copies.values() for copy in group]
    for copy in w_flat + d_done + extra + done + h_copies + list(r1.values()) + [row_copy] + r2:
        copy.wait_send()


def head_body(
    tokens,
    fine_gain,
    fine_query,
    fine_keyval,
    fine_out,
    down_weight,
    coarse_gain,
    coarse_query,
    coarse_keyval,
    coarse_out,
    up_weight,
):
    seq, tp = lax.axis_size("seq"), lax.axis_size("tp")
    rows, width = tokens.shape
    depth, local_cols = coarse_query.shape
    own = local_cols // seq
    pool_rows = rows // SHORT
    crows = pool_rows * tp
    count = crows * seq
    bf, f32 = jnp.bfloat16, jnp.float32
    V = pltpu.VMEM
    dma = lambda n: pltpu.SemaphoreType.DMA((n,))
    one = pltpu.SemaphoreType.DMA
    anywhere = pl.BlockSpec(memory_space=pl.ANY)
    vmem = pl.BlockSpec(memory_space=pltpu.VMEM)
    return pl.pallas_call(
        functools.partial(section_kernel, seq, tp),
        out_shape=jax.ShapeDtypeStruct((rows, width), bf),
        in_specs=[anywhere, vmem, anywhere, anywhere, anywhere, anywhere, vmem, anywhere,
                  anywhere, anywhere, anywhere],
        out_specs=vmem,
        scratch_shapes=[
            V((2 * rows, width), bf), V(fine_query.shape, bf), V(fine_keyval.shape, bf),
            V(fine_out.shape, bf), V((tp,) + down_weight.shape, bf), V((seq, depth, 3 * own), bf),
            V(coarse_out.shape, bf), V(up_weight.shape, bf),
            V((2 * rows, width), bf), V((rows, width), bf), V((2 * rows, 2 * width), bf),
            V((rows, width), bf), V((rows, width), bf), V((seq * tp, pool_rows, width), bf),
            V((count, tp * local_cols), bf), V((count, 3 * own), bf), V((count, 3 * own), f32),
            V((seq, crows, own), bf), V((seq, crows, own), bf), V((crows, local_cols), bf),
            V((crows, local_cols), f32), V((tp - 1, crows, local_cols), bf),
            V((tp - 1, crows, local_cols), bf), V((crows, local_cols), bf), V((16, local_cols), bf),
            V((tp - 1, pool_rows, width), bf), V((tp - 1, pool_rows, width), bf),
            dma(11), one(()), one(()), dma(3 * (seq - 1)), dma(3 * (seq - 1)), dma(tp - 1), dma(tp - 1),
            dma(seq * tp - 1), dma(seq * tp - 1), dma(seq - 1), dma(seq - 1),
            dma(tp - 1), dma(tp - 1), one(()), one(()), dma(tp - 1), dma(tp - 1),
        ],
        compiler_params=pltpu.CompilerParams(
            collective_id=0, has_side_effects=True, vmem_limit_bytes=62 * 1024 * 1024
        ),
    )(tokens, fine_gain[None], fine_query, fine_keyval, fine_out, down_weight, coarse_gain[None],
      coarse_query, jnp.transpose(coarse_keyval, (1, 0, 2)), coarse_out, up_weight)


def chosen(*args):
    seq, tp = lax.axis_size("seq"), lax.axis_size("tp")
    local_heads = args[7].shape[1] // HEAD
    powers = seq & (seq - 1) == 0 and tp & (tp - 1) == 0 and seq > 1 and tp > 1
    square = args[10].shape[0] == args[10].shape[1] == args[7].shape[1]
    if local_heads % seq == 0 and args[0].shape[0] == WINDOW and powers and square:
        return head_body(*args)
    return body(*args)


def solution(mesh):
    return jax.shard_map(
        chosen,
        mesh=mesh,
        in_specs=(
            P(("seq", "tp"), None),
            P(),
            P(),
            P(),
            P(),
            P(None, "tp"),
            P(),
            P("seq", "tp"),
            P("seq", None, "tp"),
            P("tp", None),
            P("tp", None),
        ),
        out_specs=P(("seq", "tp"), None),
        check_vma=False,
    )
```

profile of v0, /device:TPU:1, one launch (start us, length us, event | category | flops | bytes accessed | tf_op | source)
XLA Modules:
  0.0 140.1 jit_solution(17684038987049047123)
XLA Ops:
  0.0 3.6 %copy.14 = bf16[512,2,1024]{2,0,1:T(8,128)(2,1)} copy(bf16[512,2,1024]{2,1,0:T(2,128)(2,1)} %param.19) | data formatting | bytes 4194304 | tf_op args[8]
  3.6 134.6 %shard_map.109 = bf16[256,1024]{1,0:T(8,128)(2,1)} custom-call(bf16[256,1024]{1,0:T(8,128)(2,1)} %tokens.1, f32[1,1024]{1,0:T(1,128)} %bitcast.7, bf16[1024,1024]{1,0:T(8,128)(2,1)} %fine_query.1, bf16[1024,2048]{1,0:T(8,128)(2,1)} %fine_keyval.1, bf16[1024,1024]{1,0:T(8,128)(2,1)} %fine_out.1, bf16[1024,1024]{1,0:T(8,128)(2,1)} %down_weight.1, ...), custom_call_target="tpu_custom_call" | custom-call | tf_op jit(solution)/shard_map/pallas_call | solution.py:563
  138.2 1.9 %copy.16 = bf16[256,1024]{1,0:T(8,128)(2,1)} copy(bf16[256,1024]{1,0:T(8,128)(2,1)} %shard_map.109) | data formatting | bytes 1048576
where the time goes:
time: 140 us
  Pallas kernels  135 us (96%)
  local copies, waits for them, and re-layouts  5.43 us (4%)
    pallas_call x1, Pallas kernels, head_body(): pl.pallas_call(functools.partial(section_kernel, seq, tp), out_shape=jax....  135 us
    unnamed x2, local copies, waits for them, and re-layouts  5.43 us

commit v1 on v0

v1 whole, which is shorter than its diff:
```python
import functools
import math

import jax
import jax.numpy as jnp
from jax import lax
from jax.experimental import pallas as pl
from jax.experimental.pallas import tpu as pltpu
from jax.sharding import PartitionSpec as P

HEAD = 128
WINDOW = 256
SHORT = 8


epsilon = 1e-06
big_negative = -1e30


def from_behind(array, axis, by):
    size = lax.axis_size(axis)
    pairs = [(i, i + by) for i in range(size) if 0 <= i + by < size]
    return lax.ppermute(array, axis, pairs)


def normalize(values, scale_gain):
    mean_square = jnp.mean(values * values, axis=-1, keepdims=True)
    return values * lax.rsqrt(mean_square + epsilon) * scale_gain


def online_update(state, query_heads, key_piece, value_piece, query_index):
    running_max, running_sum, accumulate = state
    scale = 1.0 / math.sqrt(HEAD)
    scores = (
        jnp.einsum("qhd,khd->hqk", query_heads, key_piece, preferred_element_type=jnp.float32)
        * scale
    )
    key_index = jnp.arange(key_piece.shape[0], dtype=jnp.int32)
    allowed = key_index[None, :] <= query_index[:, None]
    scores = jnp.where(allowed[None], scores, big_negative)
    new_max = jnp.maximum(running_max, jnp.max(scores, axis=-1))
    terms = jnp.where(allowed[None], jnp.exp(scores - new_max[..., None]), 0.0)
    new_sum = jnp.sum(terms, axis=-1)
    product = jnp.einsum(
        "hqk,khd->hqd", terms.astype(jnp.bfloat16), value_piece, preferred_element_type=jnp.float32
    )
    return (new_max, new_sum, product)


def body(
    tokens,
    fine_gain,
    fine_query,
    fine_keyval,
    fine_out,
    down_weight,
    coarse_gain,
    coarse_query,
    coarse_keyval,
    coarse_out,
    up_weight,
):
    tok_rows = tokens.shape[0]
    width = tokens.shape[1]
    fine_heads = width // HEAD
    scale = 1.0 / math.sqrt(HEAD)
    start_row = lax.axis_index(("seq", "tp")) * tok_rows
    inputs = tokens.astype(jnp.float32)
    normed = normalize(inputs, fine_gain).astype(jnp.bfloat16)
    queries = jnp.dot(normed, fine_query, preferred_element_type=jnp.float32).astype(jnp.bfloat16)
    keyvals = jnp.dot(normed, fine_keyval, preferred_element_type=jnp.float32).astype(jnp.bfloat16)
    earlier = from_behind(keyvals, ("seq", "tp"), 1)
    key_rows = jnp.concatenate([earlier, keyvals], 0)
    span = key_rows.shape[0]
    key_heads = key_rows[:, :width].reshape(span, fine_heads, HEAD)
    value_heads = key_rows[:, width:].reshape(span, fine_heads, HEAD)
    query_heads = queries.reshape(tok_rows, fine_heads, HEAD)
    scores = (
        jnp.einsum("qhd,khd->hqk", query_heads, key_heads, preferred_element_type=jnp.float32)
        * scale
    )
    row_index = jnp.arange(tok_rows, dtype=jnp.int32)[:, None]
    col_index = jnp.arange(span, dtype=jnp.int32)[None, :]
    offset = row_index + WINDOW - col_index
    allowed = (offset >= 0) & (offset < WINDOW) & (start_row - WINDOW + col_index >= 0)
    scores = jnp.where(allowed[None], scores, big_negative)
    peak = jnp.max(scores, axis=-1, keepdims=True)
    terms = jnp.where(allowed[None], jnp.exp(scores - peak), 0.0)
    denom = jnp.sum(terms, axis=-1)
    mixed = jnp.einsum(
        "hqk,khd->qhd", terms.astype(jnp.bfloat16), value_heads, preferred_element_type=jnp.float32
    )
    local = (mixed / jnp.transpose(denom)[..., None]).reshape(tok_rows, width).astype(jnp.bfloat16)
    fine_state = (inputs + jnp.dot(local, fine_out, preferred_element_type=jnp.float32)).astype(
        jnp.bfloat16
    )
    pooled = jnp.mean(
        fine_state.astype(jnp.float32).reshape(tok_rows // SHORT, SHORT, width), axis=1
    ).astype(jnp.bfloat16)
    pooled_all = lax.all_gather(pooled, "tp", axis=0, tiled=True)
    short_cols = jnp.dot(pooled_all, down_weight, preferred_element_type=jnp.float32).astype(
        jnp.bfloat16
    )
    shortened = lax.all_gather(short_cols, "tp", axis=1, tiled=True)
    coarse_normed = normalize(shortened.astype(jnp.float32), coarse_gain).astype(jnp.bfloat16)
    coarse_rows = coarse_normed.shape[0]
    local_cols = coarse_query.shape[1]
    local_heads = local_cols // HEAD
    query_rows = lax.all_gather(coarse_query, "seq", axis=0, tiled=True)
    keyval_rows = lax.all_gather(coarse_keyval, "seq", axis=0, tiled=True)
    count = query_rows.shape[0]
    query_sum = jnp.dot(coarse_normed, query_rows, preferred_element_type=jnp.float32)
    keyval_sum = jnp.dot(
        coarse_normed,
        keyval_rows.reshape(count, 2 * local_cols),
        preferred_element_type=jnp.float32,
    )
    coarse_queries = query_sum.astype(jnp.bfloat16).reshape(coarse_rows, local_heads, HEAD)
    coarse_kv = keyval_sum.astype(jnp.bfloat16).reshape(coarse_rows, 2, local_cols)
    my_first = lax.axis_index("seq") * coarse_rows
    query_index = my_first + jnp.arange(coarse_rows, dtype=jnp.int32)
    initial = (
        jnp.full((local_heads, coarse_rows), big_negative, jnp.float32),
        jnp.zeros((local_heads, coarse_rows), jnp.float32),
        jnp.zeros((local_heads, coarse_rows, HEAD), jnp.float32),
    )
    piece = lax.all_gather(coarse_kv, "seq", axis=0, tiled=True)
    count = piece.shape[0]
    key_piece = piece[:, 0].reshape(count, local_heads, HEAD)
    value_piece = piece[:, 1].reshape(count, local_heads, HEAD)
    final = lax.cond(
        jnp.int32(0) < my_first + coarse_rows,
        lambda: online_update(initial, coarse_queries, key_piece, value_piece, query_index),
        lambda: initial,
    )
    head_out = final[2] / final[1][..., None]
    coarse_heads = (
        jnp.transpose(head_out, (1, 0, 2)).reshape(coarse_rows, local_cols).astype(jnp.bfloat16)
    )
    partials = jnp.dot(coarse_heads, coarse_out, preferred_element_type=jnp.float32)
    attended = lax.psum_scatter(
        partials.astype(jnp.bfloat16), "tp", scatter_dimension=1, tiled=True
    ).astype(jnp.float32)
    coarse_state = (short_cols.astype(jnp.float32) + attended).astype(jnp.bfloat16)
    prior_row = from_behind(coarse_state[coarse_rows - 1 :], "seq", 1)
    delayed = jnp.concatenate([prior_row, coarse_state[: coarse_rows - 1]], 0)
    lifted = lax.psum_scatter(
        jnp.dot(delayed, up_weight, preferred_element_type=jnp.float32).astype(jnp.bfloat16),
        "tp",
        scatter_dimension=0,
        tiled=True,
    ).astype(jnp.float32)
    result = fine_state.astype(jnp.float32) + jnp.repeat(lifted, SHORT, axis=0)
    return result.astype(jnp.bfloat16)


def flip(index, bit):
    return index + bit - 2 * bit * lax.rem(lax.div(index, jnp.int32(bit)), jnp.int32(2))


def bits_of(size):
    out, bit = [], size // 2
    while bit:
        out.append(bit)
        bit //= 2
    return out


def dot32(left, right):
    return jnp.dot(left, right, preferred_element_type=jnp.float32)


def dot_t(left, right):
    return lax.dot_general(
        left, right, (((1,), (1,)), ((), ())), preferred_element_type=jnp.float32
    )


def section_kernel(
    seq, tp,
    tokens, fine_gain, fine_query, fine_keyval, fine_out, down_weight, coarse_gain, coarse_query,
    coarse_kv, coarse_out, up_weight,
    result,
    both, wq, wkv, wo, down_own, down_g, wqk, wv, wout, wup,
    normed, queries, key_rows, local, fine_state, pooled_all, mqk, mv, pv_out, pv_in, mixed_qk,
    mixed_v, qkv, factors, terms, denoms, shifted, heads_out, heads_in, coarse_heads, short_cols,
    ss_tp, ss_seq, send1, recv1, state, send2, recv2,
    load_sem, halo_s, halo_r, qk_s, qk_r, v_s, v_r, d_s, d_r, pa_s, pa_r, pb_s, pb_r, pc_s, pc_r,
    ssa_s, ssa_r, ssb_s, ssb_r, pv_s, pv_r, h_s, h_r, r1_s, r1_r, r2_s, r2_r,
):
    me_s = lax.axis_index("seq")
    me_t = lax.axis_index("tp")
    rows, width = tokens.shape
    scale = 1.0 / math.sqrt(HEAD)
    total = seq * tp
    lin = me_s * tp + me_t
    after = lax.rem(lin + 1, total)
    before = lax.rem(lin + total - 1, total)
    bf, f32 = jnp.bfloat16, jnp.float32

    def around(index, step, size):
        return lax.rem(index + step, size)

    def toggle(index, mask):
        bit = 1
        while bit <= mask:
            if mask & bit:
                index = flip(index, bit)
            bit *= 2
        return index

    def remote(src, dst, send, recv, device):
        copy = pltpu.make_async_remote_copy(
            src_ref=src, dst_ref=dst, send_sem=send, recv_sem=recv,
            device_id=device, device_id_type=pl.DeviceIdType.MESH,
        )
        copy.start()
        return copy

    def load(src, dst, sem):
        copy = pltpu.make_async_copy(src, dst, sem)
        copy.start()
        return copy

    def arrived(dst, sem):
        pltpu.make_async_copy(dst, dst, sem).wait()

    def linear(index):
        return {"seq": lax.div(index, tp), "tp": lax.rem(index, tp)}

    depth = coarse_query.shape[0]
    own = coarse_query.shape[1] // seq
    fcols = down_own.shape[1]
    per = fcols // depth
    half = seq // 2
    zh = lax.div(me_s, half)
    in_half = lax.rem(me_s, half)
    partner = flip(me_s, half)
    pool_rows = rows // SHORT
    crows = pool_rows * tp
    count = crows * seq
    tile = 2 * HEAD

    def head_cols(dest):
        return pl.ds(pl.multiple_of(dest * own, own), own)

    barrier = pltpu.get_barrier_semaphore()
    peers = [{"seq": around(me_s, d, seq)} for d in range(1, seq)]
    peers += [{"tp": around(me_t, d, tp)} for d in range(1, tp)]
    peers += [linear(after), linear(before)]
    in_tokens = load(tokens, both.at[pl.ds(rows, rows)], load_sem.at[0])
    in_down = load(down_weight, down_own, load_sem.at[4])
    in_wq = load(fine_query, wq, load_sem.at[2])
    in_wkv = load(fine_keyval, wkv, load_sem.at[1])
    in_wo = load(fine_out, wo, load_sem.at[3])
    for pl_part, source in ((0, coarse_query), (1, coarse_kv.at[0])):
        load(source.at[:, head_cols(me_s)], wqk.at[me_s, :, pl.ds(pl_part * own, own)],
             qk_r.at[me_s])
    for k, head in enumerate((partner, me_s)):
        load(coarse_kv.at[1, :, head_cols(head)], wv.at[in_half, :, pl.ds(k * own, own)],
             v_r.at[in_half])
    in_wout = load(coarse_out, wout, load_sem.at[5])
    in_wup = load(up_weight, wup, load_sem.at[6])
    for peer in peers:
        pl.semaphore_signal(barrier, inc=1, device_id=peer, device_id_type=pl.DeviceIdType.MESH)
    pl.semaphore_wait(barrier, len(peers))

    sent = []
    halo = remote(tokens, both.at[pl.ds(0, rows)], halo_s, halo_r, linear(after))

    def send_qk(offsets):
        for d in offsets:
            dest = toggle(me_s, d)
            for k, source in enumerate((coarse_query, coarse_kv.at[0])):
                sent.append(
                    remote(
                        source.at[:, head_cols(dest)], wqk.at[me_s, :, pl.ds(k * own, own)],
                        qk_s.at[2 * (d - 1) + k], qk_r.at[me_s], {"seq": dest},
                    )
                )

    def send_v():
        for d in range(1, half):
            dest = toggle(me_s, d)
            for k, head in enumerate((flip(dest, half), dest)):
                sent.append(
                    remote(
                        coarse_kv.at[1, :, head_cols(head)],
                        wv.at[in_half, :, pl.ds(k * own, own)],
                        v_s.at[2 * (d - 1) + k], v_r.at[in_half], {"seq": dest},
                    )
                )

    tp_bits = bits_of(tp)
    send_qk(range(half, seq))

    in_down.wait()
    cgain = coarse_gain[:, pl.ds(pl.multiple_of(me_t * fcols, fcols), fcols)]
    for j in range(per):
        cols = slice(j * depth, (j + 1) * depth)
        down_g[me_t * per + j] = (down_own[:, cols].astype(f32) * cgain[:, cols]).astype(bf)

    def send_down(slot, bit, number):
        copies = []
        for j in range(per):
            block = down_g.at[slot * per + j]
            at = number * per + j
            copies.append(remote(block, block, d_s.at[at], d_r.at[at], {"tp": flip(me_t, bit)}))
        return copies

    down_copies = {bit: send_down(me_t, bit, bit - 1) for bit in tp_bits}
    send_v()
    send_qk(range(1, half))

    gain = fine_gain[...]

    def norm_rows(first):
        values = both[pl.ds(first, rows), :].astype(f32)
        normed[pl.ds(first, rows), :] = normalize(values, gain).astype(bf)

    in_tokens.wait()
    norm_rows(rows)
    in_wq.wait()

    @pl.loop(0, width // tile)
    def _(i):
        cols = pl.ds(pl.multiple_of(i * tile, tile), tile)
        queries[:, cols] = dot32(normed[rows:, :], wq[:, cols]).astype(bf)

    in_wkv.wait()

    def project_rows(first):
        @pl.loop(0, 2 * width // tile)
        def _(i):
            cols = pl.ds(pl.multiple_of(i * tile, tile), tile)
            key_rows[pl.ds(first, rows), cols] = dot32(
                normed[pl.ds(first, rows), :], wkv[:, cols]
            ).astype(bf)

    project_rows(rows)
    halo.wait()
    norm_rows(0)
    project_rows(0)

    row_index = lax.broadcasted_iota(jnp.int32, (rows, 2 * rows), 0)
    col_index = lax.broadcasted_iota(jnp.int32, (rows, 2 * rows), 1)
    offset = row_index + rows - col_index
    allowed = (offset >= 0) & (offset < WINDOW) & (lin * rows - rows + col_index >= 0)

    def weigh(query, key, mask):
        scores = jnp.where(mask, dot_t(query, key) * scale, big_negative)
        peak = jnp.max(scores, axis=-1, keepdims=True)
        weights = jnp.where(mask, jnp.exp(scores - peak), 0.0)
        return weights.astype(bf), jnp.sum(weights, axis=-1, keepdims=True)

    @pl.loop(0, width // HEAD)
    def _(h):
        cols = pl.ds(pl.multiple_of(h * HEAD, HEAD), HEAD)
        vcols = pl.ds(pl.multiple_of(width + h * HEAD, HEAD), HEAD)
        weights, denom = weigh(queries[:, cols], key_rows[:, cols], allowed)
        local[:, cols] = (dot32(weights, key_rows[:, vcols]) / denom).astype(bf)

    in_wo.wait()

    @pl.loop(0, width // tile)
    def _(i):
        cols = pl.ds(pl.multiple_of(i * tile, tile), tile)
        value = both[rows:, cols].astype(f32) + dot32(local[...], wo[:, cols])
        value = value.astype(bf)
        fine_state[:, cols] = value
        mean = jnp.mean(value.astype(f32).reshape(pool_rows, SHORT, tile), axis=1)
        pooled_all[lin, :, cols] = mean.astype(bf)

    group = []
    for d in range(1, tp):
        slot = pooled_all.at[lin]
        group.append(remote(slot, slot, pa_s.at[d - 1], pa_r.at[d - 1], {"tp": toggle(me_t, d)}))
    for copy in group:
        copy.wait_recv()
    sent.extend(group)

    core_bit = tp_bits[-1]
    share = tp // 2
    mine_first = lax.rem(me_t, 2) * share

    def blocks(first_s, offset_t):
        return pooled_all.at[pl.ds(first_s * tp + offset_t, share)]

    held = [me_s]
    number = 0
    pending = []

    def exchange(bit):
        nonlocal number, held
        copies = []
        for index in held:
            part = blocks(index, mine_first)
            copies.append(
                remote(part, part, pb_s.at[number], pb_r.at[number], {"seq": flip(me_s, bit)})
            )
            number += 1
        held = held + [flip(index, bit) for index in held]
        return copies

    seq_bits = bits_of(seq)
    pending = exchange(seq_bits[0])

    mine = pooled_all[pl.ds(me_s * tp, tp)].reshape(crows, width)
    square_sum = jnp.zeros((8, crows), f32)
    for u in range(2):
        cols = slice(u * fcols // 2, (u + 1) * fcols // 2)
        wide = dot32(mine, down_own[:, cols]).astype(bf).astype(f32)
        short_cols[pl.ds(0, crows), cols] = wide
        square_sum += lax.dot_general(
            jnp.ones((8, fcols // 2), f32), wide * wide, (((1,), (1,)), ((), ())),
            preferred_element_type=f32, precision=lax.Precision.HIGHEST,
        )
    ss_tp[me_t] = square_sum
    group = []
    for d in range(1, tp):
        slot = ss_tp.at[me_t]
        group.append(remote(slot, slot, ssa_s.at[d - 1], ssa_r.at[d - 1], {"tp": toggle(me_t, d)}))
    for copy in group:
        copy.wait_recv()
    sent.extend(group)
    whole_sum = ss_tp[0]
    for t in range(1, tp):
        whole_sum += ss_tp[t]
    ss_seq[me_s] = whole_sum
    ss_copies = []
    for d in range(1, seq):
        slot = ss_seq.at[me_s]
        ss_copies.append(
            remote(slot, slot, ssb_s.at[d - 1], ssb_r.at[d - 1], {"seq": toggle(me_s, d)})
        )
    sent.extend(ss_copies)

    for bit in seq_bits[1:] + [None]:
        for copy in pending:
            copy.wait_recv()
        sent.extend(pending)
        if bit is not None:
            pending = exchange(bit)
    pending = []
    for k, index in enumerate(held[1:]):
        part = blocks(index, mine_first)
        pending.append(
            remote(part, part, pc_s.at[k], pc_r.at[k], {"tp": flip(me_t, core_bit)})
        )
    for copy in pending:
        copy.wait_recv()
    sent.extend(pending)

    chunk = width // 4

    def add_qk(source, first):
        arrived(wqk.at[source], qk_r.at[source])

        @pl.loop(0, width // chunk)
        def _(i):
            at = pl.ds(pl.multiple_of(i * chunk, chunk), chunk)
            product = dot32(down_g[source, at, :], wqk[source])
            if first:
                mqk[at, :] = product
            else:
                mqk[at, :] += product

    started = False
    have = [0]
    for k, bit in enumerate(tp_bits):
        for copy in down_copies[bit]:
            copy.wait_recv()
        sent.extend(down_copies[bit])
        now = []
        if k + 1 < len(tp_bits):
            pass
        have.append(bit)
    for k, bit in enumerate(tp_bits[1:]):
        subs = [m for m in range(1, tp) if m % (2 * bit) == 0]
        now = []
        for sub in subs:
            now += send_down(toggle(me_t, sub), bit, bit + sub - 1)
        for copy in now:
            copy.wait_recv()
        sent.extend(now)

    for hs in range(half):
        source = zh * half + hs
        arrived(wv.at[hs], v_r.at[hs])

        @pl.loop(0, width // chunk)
        def _(i, hs=hs, source=source):
            at = pl.ds(pl.multiple_of(i * chunk, chunk), chunk)
            product = dot32(down_g[source, at, :], wv[hs])
            if hs:
                product += mv[at, :]
            mv[at, :] = product
            if hs == half - 1:
                pv_out[at, :] = product[:, :own].astype(bf)

    pv_copy = remote(pv_out, pv_in, pv_s, pv_r, {"seq": partner})
    sent.append(pv_copy)
    for e in range(tp):
        for j in range(per):
            add_qk(toggle(me_t, e) * per + j, not started)
            started = True

    mixed_qk[...] = mqk[...].astype(bf)
    for copy in ss_copies:
        copy.wait_recv()
    sums = jnp.concatenate([ss_seq[s, 0:1, :] for s in range(seq)], 0)
    inverse = lax.rsqrt(sums / (tp * fcols) + epsilon)
    turned = jnp.transpose(jnp.concatenate([inverse] * (crows // seq), 0))
    for s in range(seq):
        factors[s * crows : (s + 1) * crows, :] = jnp.broadcast_to(
            turned[:, s : s + 1], (crows, HEAD)
        )
    block = 2 * crows

    def project(columns, mixed):
        @pl.loop(0, seq // 2)
        def _(i):
            at = pl.ds(pl.multiple_of(i * block, block), block)
            pooled = pooled_all[pl.ds(i * 2 * tp, 2 * tp)].reshape(block, width)
            product = dot32(pooled, mixed[...])
            for c in range(product.shape[1] // HEAD):
                part = product[:, c * HEAD : (c + 1) * HEAD] * factors[at, :]
                first = columns + c * HEAD
                qkv[at, first : first + HEAD] = part.astype(bf)

    project(0, mixed_qk)
    for i in range(seq // 2):
        extent = (i + 1) * block
        r = lax.broadcasted_iota(jnp.int32, (block, extent), 0) + i * block
        c = lax.broadcasted_iota(jnp.int32, (block, extent), 1)
        for h in range(own // HEAD):
            part = slice(h * HEAD, (h + 1) * HEAD)
            kpart = slice(own + h * HEAD, own + (h + 1) * HEAD)
            weights, denom = weigh(qkv[i * block : extent, part], qkv[:extent, kpart], c <= r)
            terms[h, i * block : extent, :extent] = weights
            denoms[h, i * block : extent, :] = jnp.broadcast_to(denom, (block, HEAD))

    earlier = pooled_all[before_slot(me_s, tp, total), pool_rows - 16 :, :]
    for u in range(2):
        cols = slice(u * fcols // 2, (u + 1) * fcols // 2)
        last = dot32(earlier, down_own[:, cols]).astype(bf).astype(f32)[15:16, :]
        last = jnp.where(me_s > 0, last, 0.0)
        rolled = pltpu.roll(short_cols[pl.ds(0, crows), cols], 1, 0)
        top = lax.broadcasted_iota(jnp.int32, rolled.shape, 0) == 0
        short_cols[pl.ds(0, crows), cols] = jnp.where(top, last, rolled)

    pv_copy.wait_recv()
    mixed_v[...] = (mv[:, own:] + pv_in[...].astype(f32)).astype(bf)
    project(2 * own, mixed_v)
    shifted[0:1, :] = jnp.zeros((1, own), f32)
    for i in range(seq // 2):
        extent = (i + 1) * block
        for h in range(own // HEAD):
            part = slice(h * HEAD, (h + 1) * HEAD)
            vpart = slice(2 * own + h * HEAD, 2 * own + (h + 1) * HEAD)
            out = dot32(terms[h, i * block : extent, :extent], qkv[:extent, vpart])
            shifted[i * block + 1 : extent + 1, part] = out / denoms[h, i * block : extent, :]
    heads_out[...] = shifted[:count, :].astype(bf).reshape(seq, crows, own)

    heads_in[me_s] = heads_out[me_s]
    h_copies = []
    order = sorted(range(1, seq), key=lambda d: -d)
    for d in order:
        dest = toggle(me_s, d)
        h_copies.append(
            remote(
                heads_out.at[dest], heads_in.at[me_s], h_s.at[d - 1], h_r.at[d - 1],
                {"seq": dest},
            )
        )
    sent.extend(h_copies)
    in_wout.wait()
    in_wup.wait()
    for copy in h_copies:
        copy.wait_recv()
    for j in range(seq):
        coarse_heads[:, j * own : (j + 1) * own] = heads_in[j]

    def partial(t, store):
        @pl.loop(0, fcols // tile)
        def _(i):
            cols = pl.ds(pl.multiple_of(i * tile, tile), tile)
            wcols = pl.ds(pl.multiple_of(t * fcols + i * tile, tile), tile)
            store(cols, dot32(coarse_heads[...], wout[:, wcols]))

    tp_order = sorted(range(1, tp), key=lambda d: abs(2 * d - tp))
    r1 = {}
    low_bits = tp_bits[::-1]
    for k, bit in enumerate(low_bits):
        for sub in range(tp - bit, 0, -2 * bit):
            dest = toggle(me_t, sub)
            for low in low_bits[:k]:
                r1[sub + low].wait_recv()

            def put(cols, value, sub=sub, k=k):
                for low in low_bits[:k]:
                    value += recv1[sub + low - 1, :, cols].astype(f32)
                send1[sub - 1, :, cols] = value.astype(bf)

            partial(dest, put)
            r1[sub] = remote(
                send1.at[sub - 1], recv1.at[sub - 1], r1_s.at[sub - 1], r1_r.at[sub - 1],
                {"tp": flip(me_t, bit)},
            )
    sent.extend(r1.values())

    def keep(cols, value):
        short_cols[:, cols] += value

    partial(me_t, keep)
    for bit in low_bits:
        r1[bit].wait_recv()
    whole = short_cols[...]
    for bit in low_bits:
        whole += recv1[bit - 1].astype(f32)
    top = lax.broadcasted_iota(jnp.int32, whole.shape, 0) == 0
    state[...] = jnp.where(top & (me_s == 0), 0.0, whole).astype(bf)

    @pl.loop(0, width // tile)
    def _(i):
        cols = pl.ds(pl.multiple_of(i * tile, tile), tile)
        short_cols[:, cols] = dot32(state[...], wup[:, cols])

    r2 = []
    for d in tp_order:
        dest = around(me_t, d, tp)
        part = short_cols[pl.ds(pl.multiple_of(dest * pool_rows, pool_rows), pool_rows), :]
        send2[d - 1] = part.astype(bf)
        r2.append(
            remote(
                send2.at[d - 1], recv2.at[d - 1], r2_s.at[d - 1], r2_r.at[d - 1], {"tp": dest}
            )
        )
    sent.extend(r2)
    lifted = short_cols[pl.ds(pl.multiple_of(me_t * pool_rows, pool_rows), pool_rows), :]
    for copy in r2:
        copy.wait_recv()
    for d in range(1, tp):
        lifted += recv2[d - 1].astype(f32)
    spread = jnp.broadcast_to(lifted[:, None, :], (pool_rows, SHORT, width)).reshape(rows, width)
    result[...] = (fine_state[...].astype(f32) + spread).astype(bf)
    for copy in sent:
        copy.wait_send()


def before_slot(me_s, tp, total):
    return lax.rem(me_s * tp + total - 1, total)


def head_body(
    tokens,
    fine_gain,
    fine_query,
    fine_keyval,
    fine_out,
    down_weight,
    coarse_gain,
    coarse_query,
    coarse_keyval,
    coarse_out,
    up_weight,
):
    seq, tp = lax.axis_size("seq"), lax.axis_size("tp")
    rows, width = tokens.shape
    depth, local_cols = coarse_query.shape
    own = local_cols // seq
    half = seq // 2
    pool_rows = rows // SHORT
    crows = pool_rows * tp
    count = crows * seq
    bf, f32 = jnp.bfloat16, jnp.float32
    V = pltpu.VMEM
    dma = lambda n: pltpu.SemaphoreType.DMA((n,))
    one = pltpu.SemaphoreType.DMA
    anywhere = pl.BlockSpec(memory_space=pl.ANY)
    vmem = pl.BlockSpec(memory_space=pltpu.VMEM)
    return pl.pallas_call(
        functools.partial(section_kernel, seq, tp),
        out_shape=jax.ShapeDtypeStruct((rows, width), bf),
        in_specs=[anywhere, vmem, anywhere, anywhere, anywhere, anywhere, vmem, anywhere,
                  anywhere, anywhere, anywhere],
        out_specs=vmem,
        scratch_shapes=[
            V((2 * rows, width), bf), V(fine_query.shape, bf), V(fine_keyval.shape, bf),
            V(fine_out.shape, bf), V(down_weight.shape, bf), V((seq, width, depth), bf),
            V((seq, depth, 2 * own), bf), V((half, depth, 2 * own), bf),
            V(coarse_out.shape, bf), V(up_weight.shape, bf),
            V((2 * rows, width), bf), V((rows, width), bf), V((2 * rows, 2 * width), bf),
            V((rows, width), bf), V((rows, width), bf), V((seq * tp, pool_rows, width), bf),
            V((width, 2 * own), f32), V((width, 2 * own), f32), V((width, own), bf),
            V((width, own), bf), V((width, 2 * own), bf), V((width, own), bf),
            V((count, 3 * own), bf), V((count, HEAD), f32),
            V((own // HEAD, count, count), bf), V((own // HEAD, count, HEAD), f32),
            V((count + 8, own), f32), V((seq, crows, own), bf), V((seq, crows, own), bf),
            V((crows, local_cols), bf), V((crows, local_cols), f32),
            V((tp, 8, crows), f32), V((seq, 8, crows), f32),
            V((tp - 1, crows, local_cols), bf), V((tp - 1, crows, local_cols), bf),
            V((crows, local_cols), bf),
            V((tp - 1, pool_rows, width), bf), V((tp - 1, pool_rows, width), bf),
            dma(7), one(()), one(()), dma(2 * (seq - 1)), dma(seq), dma(2 * (half - 1)), dma(half),
            dma(seq - seq // tp), dma(seq - seq // tp), dma(tp - 1), dma(tp - 1),
            dma(seq - 1), dma(seq - 1), dma(seq - 1), dma(seq - 1),
            dma(tp - 1), dma(tp - 1), dma(seq - 1), dma(seq - 1), one(()), one(()),
            dma(seq - 1), dma(seq - 1), dma(tp - 1), dma(tp - 1), dma(tp - 1), dma(tp - 1),
        ],
        compiler_params=pltpu.CompilerParams(
            collective_id=0, has_side_effects=True, vmem_limit_bytes=62 * 1024 * 1024
        ),
    )(tokens, fine_gain[None], fine_query, fine_keyval, fine_out, down_weight, coarse_gain[None],
      coarse_query, jnp.transpose(coarse_keyval, (1, 0, 2)), coarse_out, up_weight)


def chosen(*args):
    seq, tp = lax.axis_size("seq"), lax.axis_size("tp")
    local_heads = args[7].shape[1] // HEAD
    powers = seq & (seq - 1) == 0 and tp & (tp - 1) == 0 and seq > 1 and tp > 1
    square = args[10].shape[0] == args[10].shape[1] == args[7].shape[1]
    paired = seq % tp == 0 and seq > 2 and args[7].shape[0] * (seq // tp) == args[7].shape[1]
    paired = paired and args[0].shape[0] // SHORT * tp == HEAD
    if local_heads % seq == 0 and args[0].shape[0] == WINDOW and powers and square and paired:
        return head_body(*args)
    return body(*args)


def solution(mesh):
    return jax.shard_map(
        chosen,
        mesh=mesh,
        in_specs=(
            P(("seq", "tp"), None),
            P(),
            P(),
            P(),
            P(),
            P(None, "tp"),
            P(),
            P("seq", "tp"),
            P("seq", None, "tp"),
            P("tp", None),
            P("tp", None),
        ),
        out_specs=P(("seq", "tp"), None),
        check_vma=False,
    )
```

time: 140 us -> 142 us (1.014)
  the two profiles are of different devices: /device:TPU:1 before, /device:TPU:9 now
where the time goes in v1:
time: 142 us
  Pallas kernels  137 us (96%)
  local copies, waits for them, and re-layouts  5.43 us (4%)
    pallas_call x1, Pallas kernels, head_body(): pl.pallas_call(functools.partial(section_kernel, seq, tp), out_shape=jax....  137 us
    unnamed x2, local copies, waits for them, and re-layouts  5.43 us

profile of v1, /device:TPU:9, one launch (start us, length us, event | category | flops | bytes accessed | tf_op | source)
XLA Modules:
  0.0 142.0 jit_solution(16325332543308608)
XLA Ops:
  0.0 3.6 %copy.14 = bf16[512,2,1024]{2,0,1:T(8,128)(2,1)} copy(bf16[512,2,1024]{2,1,0:T(2,128)(2,1)} %param.19) | data formatting | bytes 4194304 | tf_op args[8]
  3.6 136.5 %shard_map.109 = bf16[256,1024]{1,0:T(8,128)(2,1)} custom-call(bf16[256,1024]{1,0:T(8,128)(2,1)} %tokens.1, f32[1,1024]{1,0:T(1,128)} %bitcast.7, bf16[1024,1024]{1,0:T(8,128)(2,1)} %fine_query.1, bf16[1024,2048]{1,0:T(8,128)(2,1)} %fine_keyval.1, bf16[1024,1024]{1,0:T(8,128)(2,1)} %fine_out.1, bf16[1024,1024]{1,0:T(8,128)(2,1)} %down_weight.1, ...), custom_call_target="tpu_custom_call" | custom-call | tf_op jit(solution)/shard_map/pallas_call | solution.py:682
  140.1 1.9 %copy.16 = bf16[256,1024]{1,0:T(8,128)(2,1)} copy(bf16[256,1024]{1,0:T(8,128)(2,1)} %shard_map.109) | data formatting | bytes 1048576

commit v2 on v1

--- a/solution.py
+++ b/solution.py
@@ -176,13 +176,18 @@
     )
 
 
+BULK_QK = (4, 2, 4, 0, 1, 2, 3)
+BULK_V = (1, 1, 2)
+BULK_DOWN = (0, 3, 4, 5)
+
+
 def section_kernel(
     seq, tp,
     tokens, fine_gain, fine_query, fine_keyval, fine_out, down_weight, coarse_gain, coarse_query,
     coarse_kv, coarse_out, up_weight,
     result,
     both, wq, wkv, wo, down_own, down_g, wqk, wv, wout, wup,
-    normed, queries, key_rows, local, fine_state, pooled_all, mqk, mv, pv_out, pv_in, mixed_qk,
+    normed, queries, key_rows, local, fine_state, pooled_all, mv, pv_out, pv_in, mixed_qk,
     mixed_v, qkv, factors, terms, denoms, shifted, heads_out, heads_in, coarse_heads, short_cols,
     ss_tp, ss_seq, send1, recv1, state, send2, recv2,
     load_sem, halo_s, halo_r, qk_s, qk_r, v_s, v_r, d_s, d_r, pa_s, pa_r, pb_s, pb_r, pc_s, pc_r,
@@ -231,7 +236,6 @@
     depth = coarse_query.shape[0]
     own = coarse_query.shape[1] // seq
     fcols = down_own.shape[1]
-    per = fcols // depth
     half = seq // 2
     zh = lax.div(me_s, half)
     in_half = lax.rem(me_s, half)
@@ -243,6 +247,9 @@
 
     def head_cols(dest):
         return pl.ds(pl.multiple_of(dest * own, own), own)
+
+    def block_of(source):
+        return pl.ds(pl.multiple_of(source * depth, depth), depth)
 
     barrier = pltpu.get_barrier_semaphore()
     peers = [{"seq": around(me_s, d, seq)} for d in range(1, seq)]
@@ -254,10 +261,10 @@
     in_wkv = load(fine_keyval, wkv, load_sem.at[1])
     in_wo = load(fine_out, wo, load_sem.at[3])
     for pl_part, source in ((0, coarse_query), (1, coarse_kv.at[0])):
-        load(source.at[:, head_cols(me_s)], wqk.at[me_s, :, pl.ds(pl_part * own, own)],
+        load(source.at[:, head_cols(me_s)], wqk.at[block_of(me_s), pl.ds(pl_part * own, own)],
              qk_r.at[me_s])
     for k, head in enumerate((partner, me_s)):
-        load(coarse_kv.at[1, :, head_cols(head)], wv.at[in_half, :, pl.ds(k * own, own)],
+        load(coarse_kv.at[1, :, head_cols(head)], wv.at[block_of(in_half), pl.ds(k * own, own)],
              v_r.at[in_half])
     in_wout = load(coarse_out, wout, load_sem.at[5])
     in_wup = load(up_weight, wup, load_sem.at[6])
@@ -274,43 +281,82 @@
             for k, source in enumerate((coarse_query, coarse_kv.at[0])):
                 sent.append(
                     remote(
-                        source.at[:, head_cols(dest)], wqk.at[me_s, :, pl.ds(k * own, own)],
+                        source.at[:, head_cols(dest)], wqk.at[block_of(me_s), pl.ds(k * own, own)],
                         qk_s.at[2 * (d - 1) + k], qk_r.at[me_s], {"seq": dest},
                     )
                 )
 
-    def send_v():
-        for d in range(1, half):
+    def send_v(offsets):
+        for d in offsets:
             dest = toggle(me_s, d)
             for k, head in enumerate((flip(dest, half), dest)):
                 sent.append(
                     remote(
                         coarse_kv.at[1, :, head_cols(head)],
-                        wv.at[in_half, :, pl.ds(k * own, own)],
+                        wv.at[block_of(in_half), pl.ds(k * own, own)],
                         v_s.at[2 * (d - 1) + k], v_r.at[in_half], {"seq": dest},
                     )
                 )
 
     tp_bits = bits_of(tp)
-    send_qk(range(half, seq))
-
+    pieces = 4
+    span = width // pieces
     in_down.wait()
     cgain = coarse_gain[:, pl.ds(pl.multiple_of(me_t * fcols, fcols), fcols)]
-    for j in range(per):
-        cols = slice(j * depth, (j + 1) * depth)
-        down_g[me_t * per + j] = (down_own[:, cols].astype(f32) * cgain[:, cols]).astype(bf)
-
-    def send_down(slot, bit, number):
-        copies = []
-        for j in range(per):
-            block = down_g.at[slot * per + j]
-            at = number * per + j
-            copies.append(remote(block, block, d_s.at[at], d_r.at[at], {"tp": flip(me_t, bit)}))
-        return copies
-
-    down_copies = {bit: send_down(me_t, bit, bit - 1) for bit in tp_bits}
-    send_v()
-    send_qk(range(1, half))
+
+    def slot_cols(slot):
+        return pl.ds(pl.multiple_of(slot * fcols, fcols), fcols)
+
+    def down_piece(slot, bit, number, r):
+        part = down_g.at[pl.ds(r * span, span), slot_cols(slot)]
+        at = number * pieces + r
+        return remote(part, part, d_s.at[at], d_r.at[at], {"tp": flip(me_t, bit)})
+
+    direct = {}
+
+    def launch_down(r):
+        at = pl.ds(r * span, span)
+        down_g[at, slot_cols(me_t)] = (down_own[at, :].astype(f32) * cgain).astype(bf)
+        for bit in tp_bits:
+            direct[r, bit] = down_piece(me_t, bit, bit - 1, r)
+
+    def forward_down(r):
+        direct[r, tp_bits[0]].wait_recv()
+        for bit in tp_bits[1:]:
+            if bit != tp_bits[1]:
+                for copy in later[r]:
+                    copy.wait_recv()
+            later.setdefault(r, []).extend(
+                down_piece(toggle(me_t, sub), bit, bit + sub - 1, r)
+                for sub in range(2 * bit, tp, 2 * bit)
+            )
+            later[r].append(direct[r, bit])
+
+    later = {}
+
+    def finish_down(r):
+        for copy in later[r]:
+            copy.wait_recv()
+        sent.extend(later[r] + [direct[r, tp_bits[0]]])
+
+    bulk = {}
+    for d in range(1, seq):
+        bulk.setdefault(BULK_QK[d - 1] if seq == 8 else 0, []).append(("qk", d))
+    for d in range(1, half):
+        bulk.setdefault(BULK_V[d - 1] if seq == 8 else 0, []).append(("v", d))
+    for r in range(pieces):
+        bulk.setdefault(BULK_DOWN[r], []).append(("down", r))
+
+    def issue(stage):
+        for kind, d in bulk.get(stage, []):
+            if kind == "qk":
+                send_qk([d])
+            elif kind == "v":
+                send_v([d])
+            else:
+                launch_down(d)
+
+    issue(0)
 
     gain = fine_gain[...]
 
@@ -338,9 +384,11 @@
             ).astype(bf)
 
     project_rows(rows)
+    issue(1)
     halo.wait()
     norm_rows(0)
     project_rows(0)
+    issue(2)
 
     row_index = lax.broadcasted_iota(jnp.int32, (rows, 2 * rows), 0)
     col_index = lax.broadcasted_iota(jnp.int32, (rows, 2 * rows), 1)
@@ -375,6 +423,7 @@
     for d in range(1, tp):
         slot = pooled_all.at[lin]
         group.append(remote(slot, slot, pa_s.at[d - 1], pa_r.at[d - 1], {"tp": toggle(me_t, d)}))
+    issue(3)
     for copy in group:
         copy.wait_recv()
     sent.extend(group)
@@ -386,24 +435,20 @@
     def blocks(first_s, offset_t):
         return pooled_all.at[pl.ds(first_s * tp + offset_t, share)]
 
-    held = [me_s]
-    number = 0
-    pending = []
-
-    def exchange(bit):
-        nonlocal number, held
-        copies = []
-        for index in held:
-            part = blocks(index, mine_first)
-            copies.append(
-                remote(part, part, pb_s.at[number], pb_r.at[number], {"seq": flip(me_s, bit)})
-            )
-            number += 1
-        held = held + [flip(index, bit) for index in held]
-        return copies
-
     seq_bits = bits_of(seq)
-    pending = exchange(seq_bits[0])
+    gather = {}
+
+    def spread_block(mask):
+        for bit in seq_bits:
+            if mask == 0 or bit < (mask & -mask):
+                part = blocks(toggle(me_s, mask), mine_first)
+                at = (mask | bit) - 1
+                gather[at + 1] = remote(
+                    part, part, pb_s.at[at], pb_r.at[at], {"seq": flip(me_s, bit)}
+                )
+
+    spread_block(0)
+    issue(4)
 
     mine = pooled_all[pl.ds(me_s * tp, tp)].reshape(crows, width)
     square_sum = jnp.zeros((8, crows), f32)
@@ -420,6 +465,14 @@
     for d in range(1, tp):
         slot = ss_tp.at[me_t]
         group.append(remote(slot, slot, ssa_s.at[d - 1], ssa_r.at[d - 1], {"tp": toggle(me_t, d)}))
+    evens = sorted(range(2, seq, 2), key=lambda m: (bin(m).count("1"), m))
+    for at, mask in enumerate(evens):
+        gather[mask].wait_recv()
+        spread_block(mask)
+        issue(5 + at)
+
+    for piece in range(pieces):
+        forward_down(piece)
     for copy in group:
         copy.wait_recv()
     sent.extend(group)
@@ -434,16 +487,27 @@
             remote(slot, slot, ssb_s.at[d - 1], ssb_r.at[d - 1], {"seq": toggle(me_s, d)})
         )
     sent.extend(ss_copies)
-
-    for bit in seq_bits[1:] + [None]:
-        for copy in pending:
-            copy.wait_recv()
-        sent.extend(pending)
-        if bit is not None:
-            pending = exchange(bit)
+    for hs in range(half):
+        arrived(wv.at[pl.ds(hs * depth, depth)], v_r.at[hs])
+    half_cols = pl.ds(pl.multiple_of(zh * half * depth, half * depth), half * depth)
+    pv_copies = []
+    for piece in range(pieces):
+        finish_down(piece)
+        at = slice(piece * span, (piece + 1) * span)
+        product = dot32(down_g[at, half_cols], wv[...])
+        pv_out[at, :] = product[:, :own].astype(bf)
+        mv[at, :] = product[:, own:]
+        at = pl.ds(piece * span, span)
+        pv_copies.append(
+            remote(pv_out.at[at], pv_in.at[at], pv_s.at[piece], pv_r.at[piece], {"seq": partner})
+        )
+    sent.extend(pv_copies)
+    for mask in range(1, seq, 2):
+        gather[mask].wait_recv()
+    sent.extend(gather.values())
     pending = []
-    for k, index in enumerate(held[1:]):
-        part = blocks(index, mine_first)
+    for k in range(seq - 1):
+        part = blocks(toggle(me_s, k + 1), mine_first)
         pending.append(
             remote(part, part, pc_s.at[k], pc_r.at[k], {"tp": flip(me_t, core_bit)})
         )
@@ -451,61 +515,14 @@
         copy.wait_recv()
     sent.extend(pending)
 
-    chunk = width // 4
-
-    def add_qk(source, first):
-        arrived(wqk.at[source], qk_r.at[source])
-
-        @pl.loop(0, width // chunk)
-        def _(i):
-            at = pl.ds(pl.multiple_of(i * chunk, chunk), chunk)
-            product = dot32(down_g[source, at, :], wqk[source])
-            if first:
-                mqk[at, :] = product
-            else:
-                mqk[at, :] += product
-
-    started = False
-    have = [0]
-    for k, bit in enumerate(tp_bits):
-        for copy in down_copies[bit]:
-            copy.wait_recv()
-        sent.extend(down_copies[bit])
-        now = []
-        if k + 1 < len(tp_bits):
-            pass
-        have.append(bit)
-    for k, bit in enumerate(tp_bits[1:]):
-        subs = [m for m in range(1, tp) if m % (2 * bit) == 0]
-        now = []
-        for sub in subs:
-            now += send_down(toggle(me_t, sub), bit, bit + sub - 1)
-        for copy in now:
-            copy.wait_recv()
-        sent.extend(now)
-
-    for hs in range(half):
-        source = zh * half + hs
-        arrived(wv.at[hs], v_r.at[hs])
-
-        @pl.loop(0, width // chunk)
-        def _(i, hs=hs, source=source):
-            at = pl.ds(pl.multiple_of(i * chunk, chunk), chunk)
-            product = dot32(down_g[source, at, :], wv[hs])
-            if hs:
-                product += mv[at, :]
-            mv[at, :] = product
-            if hs == half - 1:
-                pv_out[at, :] = product[:, :own].astype(bf)
-
-    pv_copy = remote(pv_out, pv_in, pv_s, pv_r, {"seq": partner})
-    sent.append(pv_copy)
-    for e in range(tp):
-        for j in range(per):
-            add_qk(toggle(me_t, e) * per + j, not started)
-            started = True
-
-    mixed_qk[...] = mqk[...].astype(bf)
+    for source in range(seq):
+        arrived(wqk.at[pl.ds(source * depth, depth)], qk_r.at[source])
+
+    @pl.loop(0, pieces)
+    def _(i):
+        at = pl.ds(pl.multiple_of(i * span, span), span)
+        mixed_qk[at, :] = dot32(down_g[at, :], wqk[...]).astype(bf)
+
     for copy in ss_copies:
         copy.wait_recv()
     sums = jnp.concatenate([ss_seq[s, 0:1, :] for s in range(seq)], 0)
@@ -549,8 +566,9 @@
         top = lax.broadcasted_iota(jnp.int32, rolled.shape, 0) == 0
         short_cols[pl.ds(0, crows), cols] = jnp.where(top, last, rolled)
 
-    pv_copy.wait_recv()
-    mixed_v[...] = (mv[:, own:] + pv_in[...].astype(f32)).astype(bf)
+    for copy in pv_copies:
+        copy.wait_recv()
+    mixed_v[...] = (mv[...] + pv_in[...].astype(f32)).astype(bf)
     project(2 * own, mixed_v)
     shifted[0:1, :] = jnp.zeros((1, own), f32)
     for i in range(seq // 2):
@@ -687,12 +705,12 @@
         out_specs=vmem,
         scratch_shapes=[
             V((2 * rows, width), bf), V(fine_query.shape, bf), V(fine_keyval.shape, bf),
-            V(fine_out.shape, bf), V(down_weight.shape, bf), V((seq, width, depth), bf),
-            V((seq, depth, 2 * own), bf), V((half, depth, 2 * own), bf),
+            V(fine_out.shape, bf), V(down_weight.shape, bf), V((width, seq * depth), bf),
+            V((seq * depth, 2 * own), bf), V((half * depth, 2 * own), bf),
             V(coarse_out.shape, bf), V(up_weight.shape, bf),
             V((2 * rows, width), bf), V((rows, width), bf), V((2 * rows, 2 * width), bf),
             V((rows, width), bf), V((rows, width), bf), V((seq * tp, pool_rows, width), bf),
-            V((width, 2 * own), f32), V((width, 2 * own), f32), V((width, own), bf),
+            V((width, own), f32), V((width, own), bf),
             V((width, own), bf), V((width, 2 * own), bf), V((width, own), bf),
             V((count, 3 * own), bf), V((count, HEAD), f32),
             V((own // HEAD, count, count), bf), V((own // HEAD, count, HEAD), f32),
@@ -703,9 +721,9 @@
             V((crows, local_cols), bf),
             V((tp - 1, pool_rows, width), bf), V((tp - 1, pool_rows, width), bf),
             dma(7), one(()), one(()), dma(2 * (seq - 1)), dma(seq), dma(2 * (half - 1)), dma(half),
-            dma(seq - seq // tp), dma(seq - seq // tp), dma(tp - 1), dma(tp - 1),
+            dma(4 * (tp - 1)), dma(4 * (tp - 1)), dma(tp - 1), dma(tp - 1),
             dma(seq - 1), dma(seq - 1), dma(seq - 1), dma(seq - 1),
-            dma(tp - 1), dma(tp - 1), dma(seq - 1), dma(seq - 1), one(()), one(()),
+            dma(tp - 1), dma(tp - 1), dma(seq - 1), dma(seq - 1), dma(4), dma(4),
             dma(seq - 1), dma(seq - 1), dma(tp - 1), dma(tp - 1), dma(tp - 1), dma(tp - 1),
         ],
         compiler_params=pltpu.CompilerParams(

time: 142 us -> 115 us (0.81)
  the two profiles are of different devices: /device:TPU:9 before, /device:TPU:19 now
where the time goes in v2:
time: 115 us; the launch traced here: 114 us
  Pallas kernels  109 us (95%)
  local copies, waits for them, and re-layouts  5.43 us (5%)
    pallas_call x1, Pallas kernels, head_body(): pl.pallas_call(functools.partial(section_kernel, seq, tp), out_shape=jax....  109 us
    unnamed x2, local copies, waits for them, and re-layouts  5.43 us

profile of v2, /device:TPU:19, one launch (start us, length us, event | category | flops | bytes accessed | tf_op | source)
XLA Modules:
  0.0 114.5 jit_solution(2768666398674512876)
XLA Ops:
  0.0 3.6 %copy.14 = bf16[512,2,1024]{2,0,1:T(8,128)(2,1)} copy(bf16[512,2,1024]{2,1,0:T(2,128)(2,1)} %param.19) | data formatting | bytes 4194304 | tf_op args[8]
  3.6 109.0 %shard_map.109 = bf16[256,1024]{1,0:T(8,128)(2,1)} custom-call(bf16[256,1024]{1,0:T(8,128)(2,1)} %tokens.1, f32[1,1024]{1,0:T(1,128)} %bitcast.7, bf16[1024,1024]{1,0:T(8,128)(2,1)} %fine_query.1, bf16[1024,2048]{1,0:T(8,128)(2,1)} %fine_keyval.1, bf16[1024,1024]{1,0:T(8,128)(2,1)} %fine_out.1, bf16[1024,1024]{1,0:T(8,128)(2,1)} %down_weight.1, ...), custom_call_target="tpu_custom_call" | custom-call | tf_op jit(solution)/shard_map/pallas_call | solution.py:700
  112.6 1.9 %copy.16 = bf16[256,1024]{1,0:T(8,128)(2,1)} copy(bf16[256,1024]{1,0:T(8,128)(2,1)} %shard_map.109) | data formatting | bytes 1048576

commit v3 on v2

--- a/solution.py
+++ b/solution.py
@@ -176,9 +176,16 @@
     )
 
 
-BULK_QK = (4, 2, 4, 0, 1, 2, 3)
-BULK_V = (1, 1, 2)
-BULK_DOWN = (0, 3, 4, 5)
+PLAN = (
+    (("down", 0), ("qk", 4)),
+    (("v", 3), ("v", 1), ("v", 2), ("qk", 6), ("qk", 1)),
+    (),
+    (("down", 1),),
+    (("qk", 5), ("qk", 2), ("down", 2)),
+    (("down", 3),),
+    (("qk", 7), ("qk", 3)),
+    (),
+)
 
 
 def section_kernel(
@@ -188,7 +195,7 @@
     result,
     both, wq, wkv, wo, down_own, down_g, wqk, wv, wout, wup,
     normed, queries, key_rows, local, fine_state, pooled_all, mv, pv_out, pv_in, mixed_qk,
-    mixed_v, qkv, factors, terms, denoms, shifted, heads_out, heads_in, coarse_heads, short_cols,
+    mixed_v, qkv, factors, shifted, heads_out, heads_in, coarse_heads, short_cols, lift,
     ss_tp, ss_seq, send1, recv1, state, send2, recv2,
     load_sem, halo_s, halo_r, qk_s, qk_r, v_s, v_r, d_s, d_r, pa_s, pa_r, pb_s, pb_r, pc_s, pc_r,
     ssa_s, ssa_r, ssb_s, ssb_r, pv_s, pv_r, h_s, h_r, r1_s, r1_r, r2_s, r2_r,
@@ -339,16 +346,13 @@
             copy.wait_recv()
         sent.extend(later[r] + [direct[r, tp_bits[0]]])
 
-    bulk = {}
-    for d in range(1, seq):
-        bulk.setdefault(BULK_QK[d - 1] if seq == 8 else 0, []).append(("qk", d))
-    for d in range(1, half):
-        bulk.setdefault(BULK_V[d - 1] if seq == 8 else 0, []).append(("v", d))
-    for r in range(pieces):
-        bulk.setdefault(BULK_DOWN[r], []).append(("down", r))
+    plan = PLAN
+    if sum(len(stage) for stage in PLAN) != seq - 1 + half - 1 + pieces:
+        plan = [[("qk", d) for d in range(1, seq)] + [("v", d) for d in range(1, half)]]
+        plan[0] += [("down", r) for r in range(pieces)]
 
     def issue(stage):
-        for kind, d in bulk.get(stage, []):
+        for kind, d in plan[stage] if stage < len(plan) else ():
             if kind == "qk":
                 send_qk([d])
             elif kind == "v":
@@ -385,7 +389,8 @@
 
     project_rows(rows)
     issue(1)
-    halo.wait()
+    halo.wait_recv()
+    sent.append(halo)
     norm_rows(0)
     project_rows(0)
     issue(2)
@@ -546,16 +551,6 @@
                 qkv[at, first : first + HEAD] = part.astype(bf)
 
     project(0, mixed_qk)
-    for i in range(seq // 2):
-        extent = (i + 1) * block
-        r = lax.broadcasted_iota(jnp.int32, (block, extent), 0) + i * block
-        c = lax.broadcasted_iota(jnp.int32, (block, extent), 1)
-        for h in range(own // HEAD):
-            part = slice(h * HEAD, (h + 1) * HEAD)
-            kpart = slice(own + h * HEAD, own + (h + 1) * HEAD)
-            weights, denom = weigh(qkv[i * block : extent, part], qkv[:extent, kpart], c <= r)
-            terms[h, i * block : extent, :extent] = weights
-            denoms[h, i * block : extent, :] = jnp.broadcast_to(denom, (block, HEAD))
 
     earlier = pooled_all[before_slot(me_s, tp, total), pool_rows - 16 :, :]
     for u in range(2):
@@ -571,58 +566,70 @@
     mixed_v[...] = (mv[...] + pv_in[...].astype(f32)).astype(bf)
     project(2 * own, mixed_v)
     shifted[0:1, :] = jnp.zeros((1, own), f32)
+
+    def heads_copy(index):
+        return pltpu.make_async_remote_copy(
+            src_ref=heads_out.at[index], dst_ref=heads_in.at[me_s], send_sem=h_s.at[index],
+            recv_sem=h_r.at[me_s], device_id={"seq": index}, device_id_type=pl.DeviceIdType.MESH,
+        )
+
     for i in range(seq // 2):
         extent = (i + 1) * block
+        r = lax.broadcasted_iota(jnp.int32, (block, extent), 0) + i * block
+        c = lax.broadcasted_iota(jnp.int32, (block, extent), 1)
         for h in range(own // HEAD):
             part = slice(h * HEAD, (h + 1) * HEAD)
+            kpart = slice(own + h * HEAD, own + (h + 1) * HEAD)
             vpart = slice(2 * own + h * HEAD, 2 * own + (h + 1) * HEAD)
-            out = dot32(terms[h, i * block : extent, :extent], qkv[:extent, vpart])
-            shifted[i * block + 1 : extent + 1, part] = out / denoms[h, i * block : extent, :]
-    heads_out[...] = shifted[:count, :].astype(bf).reshape(seq, crows, own)
+            weights, denom = weigh(qkv[i * block : extent, part], qkv[:extent, kpart], c <= r)
+            out = dot32(weights, qkv[:extent, vpart]) / denom
+            shifted[i * block + 1 : extent + 1, part] = out
+        for index in (2 * i, 2 * i + 1):
+            heads_out[index] = shifted[index * crows : (index + 1) * crows, :].astype(bf)
+
+            @pl.when(me_s != index)
+            def _(index=index):
+                heads_copy(index).start()
 
     heads_in[me_s] = heads_out[me_s]
-    h_copies = []
-    order = sorted(range(1, seq), key=lambda d: -d)
-    for d in order:
-        dest = toggle(me_s, d)
-        h_copies.append(
-            remote(
-                heads_out.at[dest], heads_in.at[me_s], h_s.at[d - 1], h_r.at[d - 1],
-                {"seq": dest},
-            )
-        )
-    sent.extend(h_copies)
     in_wout.wait()
     in_wup.wait()
-    for copy in h_copies:
-        copy.wait_recv()
     for j in range(seq):
+
+        @pl.when(me_s != j)
+        def _(j=j):
+            arrived(heads_in.at[j], h_r.at[j])
+
         coarse_heads[:, j * own : (j + 1) * own] = heads_in[j]
 
-    def partial(t, store):
-        @pl.loop(0, fcols // tile)
+    sides = 2
+    side = fcols // sides
+
+    def partial(t, u, store):
+        @pl.loop(0, side // tile)
         def _(i):
-            cols = pl.ds(pl.multiple_of(i * tile, tile), tile)
-            wcols = pl.ds(pl.multiple_of(t * fcols + i * tile, tile), tile)
+            cols = pl.ds(pl.multiple_of(u * side + i * tile, tile), tile)
+            wcols = pl.ds(pl.multiple_of(t * fcols + u * side + i * tile, tile), tile)
             store(cols, dot32(coarse_heads[...], wout[:, wcols]))
 
-    tp_order = sorted(range(1, tp), key=lambda d: abs(2 * d - tp))
     r1 = {}
-    low_bits = tp_bits[::-1]
-    for k, bit in enumerate(low_bits):
-        for sub in range(tp - bit, 0, -2 * bit):
-            dest = toggle(me_t, sub)
-            for low in low_bits[:k]:
-                r1[sub + low].wait_recv()
-
-            def put(cols, value, sub=sub, k=k):
-                for low in low_bits[:k]:
+    for sub in range(tp - 1, 0, -1):
+        bit = sub & -sub
+        lows = [low for low in tp_bits if low < bit]
+        for u in range(sides):
+            ucols = pl.ds(u * side, side)
+            for low in lows:
+                r1[sub + low, u].wait_recv()
+
+            def put(cols, value, sub=sub, lows=lows):
+                for low in lows:
                     value += recv1[sub + low - 1, :, cols].astype(f32)
                 send1[sub - 1, :, cols] = value.astype(bf)
 
-            partial(dest, put)
-            r1[sub] = remote(
-                send1.at[sub - 1], recv1.at[sub - 1], r1_s.at[sub - 1], r1_r.at[sub - 1],
+            partial(toggle(me_t, sub), u, put)
+            at = (sub - 1) * sides + u
+            r1[sub, u] = remote(
+                send1.at[sub - 1, :, ucols], recv1.at[sub - 1, :, ucols], r1_s.at[at], r1_r.at[at],
                 {"tp": flip(me_t, bit)},
             )
     sent.extend(r1.values())
@@ -630,38 +637,53 @@
     def keep(cols, value):
         short_cols[:, cols] += value
 
-    partial(me_t, keep)
-    for bit in low_bits:
-        r1[bit].wait_recv()
-    whole = short_cols[...]
-    for bit in low_bits:
-        whole += recv1[bit - 1].astype(f32)
-    top = lax.broadcasted_iota(jnp.int32, whole.shape, 0) == 0
-    state[...] = jnp.where(top & (me_s == 0), 0.0, whole).astype(bf)
-
-    @pl.loop(0, width // tile)
-    def _(i):
-        cols = pl.ds(pl.multiple_of(i * tile, tile), tile)
-        short_cols[:, cols] = dot32(state[...], wup[:, cols])
-
+    for u in range(sides):
+        partial(me_t, u, keep)
+    tp_order = sorted(range(1, tp), key=lambda d: abs(2 * d - tp))
     r2 = []
-    for d in tp_order:
-        dest = around(me_t, d, tp)
-        part = short_cols[pl.ds(pl.multiple_of(dest * pool_rows, pool_rows), pool_rows), :]
-        send2[d - 1] = part.astype(bf)
-        r2.append(
-            remote(
-                send2.at[d - 1], recv2.at[d - 1], r2_s.at[d - 1], r2_r.at[d - 1], {"tp": dest}
-            )
-        )
+    for u in range(sides):
+        ucols = slice(u * side, (u + 1) * side)
+        for bit in tp_bits:
+            r1[bit, u].wait_recv()
+        whole = short_cols[:, ucols]
+        for bit in tp_bits:
+            whole += recv1[bit - 1, :, ucols].astype(f32)
+        top = lax.broadcasted_iota(jnp.int32, whole.shape, 0) == 0
+        state[:, ucols] = jnp.where(top & (me_s == 0), 0.0, whole).astype(bf)
+        for w in range(sides):
+            wcols = slice(w * width // sides, (w + 1) * width // sides)
+            product = dot32(state[:, ucols], wup[ucols, wcols])
+            if u:
+                product += lift[:, wcols]
+            lift[:, wcols] = product
+            if u == sides - 1:
+                for d in tp_order:
+                    dest = around(me_t, d, tp)
+                    some = pl.ds(pl.multiple_of(dest * pool_rows, pool_rows), pool_rows)
+                    at = (d - 1) * sides + w
+                    send2[at] = lift[some, wcols].astype(bf)
+                    r2.append(
+                        remote(
+                            send2.at[at], recv2.at[at], r2_s.at[at], r2_r.at[at], {"tp": dest}
+                        )
+                    )
     sent.extend(r2)
-    lifted = short_cols[pl.ds(pl.multiple_of(me_t * pool_rows, pool_rows), pool_rows), :]
-    for copy in r2:
-        copy.wait_recv()
-    for d in range(1, tp):
-        lifted += recv2[d - 1].astype(f32)
-    spread = jnp.broadcast_to(lifted[:, None, :], (pool_rows, SHORT, width)).reshape(rows, width)
-    result[...] = (fine_state[...].astype(f32) + spread).astype(bf)
+    for w in range(sides):
+        wcols = slice(w * width // sides, (w + 1) * width // sides)
+        for copy in r2[w * (tp - 1) : (w + 1) * (tp - 1)]:
+            copy.wait_recv()
+        lifted = lift[pl.ds(pl.multiple_of(me_t * pool_rows, pool_rows), pool_rows), wcols]
+        for d in range(1, tp):
+            lifted += recv2[(d - 1) * sides + w].astype(f32)
+        spread = jnp.broadcast_to(lifted[:, None, :], (pool_rows, SHORT, width // sides))
+        spread = spread.reshape(rows, width // sides)
+        result[:, wcols] = (fine_state[:, wcols].astype(f32) + spread).astype(bf)
+    for index in range(seq):
+
+        @pl.when(me_s != index)
+        def _(index=index):
+            heads_copy(index).wait_send()
+
     for copy in sent:
         copy.wait_send()
 
@@ -713,18 +735,18 @@
             V((width, own), f32), V((width, own), bf),
             V((width, own), bf), V((width, 2 * own), bf), V((width, own), bf),
             V((count, 3 * own), bf), V((count, HEAD), f32),
-            V((own // HEAD, count, count), bf), V((own // HEAD, count, HEAD), f32),
             V((count + 8, own), f32), V((seq, crows, own), bf), V((seq, crows, own), bf),
-            V((crows, local_cols), bf), V((crows, local_cols), f32),
+            V((crows, local_cols), bf), V((crows, local_cols), f32), V((crows, width), f32),
             V((tp, 8, crows), f32), V((seq, 8, crows), f32),
             V((tp - 1, crows, local_cols), bf), V((tp - 1, crows, local_cols), bf),
             V((crows, local_cols), bf),
-            V((tp - 1, pool_rows, width), bf), V((tp - 1, pool_rows, width), bf),
+            V((2 * (tp - 1), pool_rows, width // 2), bf), V((2 * (tp - 1), pool_rows, width // 2), bf),
             dma(7), one(()), one(()), dma(2 * (seq - 1)), dma(seq), dma(2 * (half - 1)), dma(half),
             dma(4 * (tp - 1)), dma(4 * (tp - 1)), dma(tp - 1), dma(tp - 1),
             dma(seq - 1), dma(seq - 1), dma(seq - 1), dma(seq - 1),
             dma(tp - 1), dma(tp - 1), dma(seq - 1), dma(seq - 1), dma(4), dma(4),
-            dma(seq - 1), dma(seq - 1), dma(tp - 1), dma(tp - 1), dma(tp - 1), dma(tp - 1),
+            dma(seq), dma(seq), dma(2 * (tp - 1)), dma(2 * (tp - 1)), dma(2 * (tp - 1)),
+            dma(2 * (tp - 1)),
         ],
         compiler_params=pltpu.CompilerParams(
             collective_id=0, has_side_effects=True, vmem_limit_bytes=62 * 1024 * 1024

time: 115 us -> 106 us (0.922)
  Pallas kernels: 109 us -> 100 us
    pallas_call x1, Pallas kernels: 109 us -> 100 us  [head_body(): pl.pallas_call(functools.partial(section_kernel, seq, tp), out_shape=jax....]
where the time goes in v3:
time: 106 us; the launch traced here: 105 us
  Pallas kernels  100 us (94%)
  local copies, waits for them, and re-layouts  5.43 us (5%)
    pallas_call x1, Pallas kernels, head_body(): pl.pallas_call(functools.partial(section_kernel, seq, tp), out_shape=jax....  100 us
    unnamed x2, local copies, waits for them, and re-layouts  5.43 us

profile of v3, /device:TPU:19, one launch (start us, length us, event | category | flops | bytes accessed | tf_op | source)
XLA Modules:
  0.0 105.4 jit_solution(17454706516095133774)
XLA Ops:
  0.0 3.6 %copy.14 = bf16[512,2,1024]{2,0,1:T(8,128)(2,1)} copy(bf16[512,2,1024]{2,1,0:T(2,128)(2,1)} %param.19) | data formatting | bytes 4194304 | tf_op args[8]
  3.6 100.0 %shard_map.109 = bf16[256,1024]{1,0:T(8,128)(2,1)} custom-call(bf16[256,1024]{1,0:T(8,128)(2,1)} %tokens.1, f32[1,1024]{1,0:T(1,128)} %bitcast.7, bf16[1024,1024]{1,0:T(8,128)(2,1)} %fine_query.1, bf16[1024,2048]{1,0:T(8,128)(2,1)} %fine_keyval.1, bf16[1024,1024]{1,0:T(8,128)(2,1)} %fine_out.1, bf16[1024,1024]{1,0:T(8,128)(2,1)} %down_weight.1, ...), custom_call_target="tpu_custom_call" | custom-call | tf_op jit(solution)/shard_map/pallas_call | solution.py:722
  103.6 1.9 %copy.16 = bf16[256,1024]{1,0:T(8,128)(2,1)} copy(bf16[256,1024]{1,0:T(8,128)(2,1)} %shard_map.109) | data formatting | bytes 1048576

commit v4 on v3

--- a/solution.py
+++ b/solution.py
@@ -181,7 +181,8 @@
     (("v", 3), ("v", 1), ("v", 2), ("qk", 6), ("qk", 1)),
     (),
     (("down", 1),),
-    (("qk", 5), ("qk", 2), ("down", 2)),
+    (("qk", 5), ("qk", 2)),
+    (("down", 2),),
     (("down", 3),),
     (("qk", 7), ("qk", 3)),
     (),
@@ -193,7 +194,7 @@
     tokens, fine_gain, fine_query, fine_keyval, fine_out, down_weight, coarse_gain, coarse_query,
     coarse_kv, coarse_out, up_weight,
     result,
-    both, wq, wkv, wo, down_own, down_g, wqk, wv, wout, wup,
+    kv_raw, kv, both, wq, wkv, wo, down_own, down_g, wqk, wv, wout, wup,
     normed, queries, key_rows, local, fine_state, pooled_all, mv, pv_out, pv_in, mixed_qk,
     mixed_v, qkv, factors, shifted, heads_out, heads_in, coarse_heads, short_cols, lift,
     ss_tp, ss_seq, send1, recv1, state, send2, recv2,
@@ -262,22 +263,37 @@
     peers = [{"seq": around(me_s, d, seq)} for d in range(1, seq)]
     peers += [{"tp": around(me_t, d, tp)} for d in range(1, tp)]
     peers += [linear(after), linear(before)]
+    in_kv = load(coarse_kv, kv_raw, load_sem.at[5])
+    in_down = load(down_weight, down_own, load_sem.at[4])
     in_tokens = load(tokens, both.at[pl.ds(rows, rows)], load_sem.at[0])
-    in_down = load(down_weight, down_own, load_sem.at[4])
+    load(coarse_query.at[:, head_cols(me_s)], wqk.at[block_of(me_s), pl.ds(0, own)], qk_r.at[me_s])
+    for peer in peers:
+        pl.semaphore_signal(barrier, inc=1, device_id=peer, device_id_type=pl.DeviceIdType.MESH)
+    in_kv.wait()
     in_wq = load(fine_query, wq, load_sem.at[2])
     in_wkv = load(fine_keyval, wkv, load_sem.at[1])
     in_wo = load(fine_out, wo, load_sem.at[3])
-    for pl_part, source in ((0, coarse_query), (1, coarse_kv.at[0])):
-        load(source.at[:, head_cols(me_s)], wqk.at[block_of(me_s), pl.ds(pl_part * own, own)],
-             qk_r.at[me_s])
+    step = HEAD
+    picks = []
+    for k in range(2):
+        r = lax.broadcasted_iota(jnp.int32, (step, 2 * step), 0)
+        c = lax.broadcasted_iota(jnp.int32, (step, 2 * step), 1)
+        picks.append((c == 2 * r + k).astype(bf))
+
+    @pl.loop(0, depth // step, unroll=2)
+    def _(i):
+        at = pl.ds(pl.multiple_of(i * step, step), step)
+        turns = kv_raw[at].reshape(2 * step, kv_raw.shape[2])
+        for k in range(2):
+            kv[k, at, :] = dot32(picks[k], turns).astype(bf)
+
+    load(kv.at[0, :, head_cols(me_s)], wqk.at[block_of(me_s), pl.ds(own, own)], qk_r.at[me_s])
     for k, head in enumerate((partner, me_s)):
-        load(coarse_kv.at[1, :, head_cols(head)], wv.at[block_of(in_half), pl.ds(k * own, own)],
+        load(kv.at[1, :, head_cols(head)], wv.at[block_of(in_half), pl.ds(k * own, own)],
              v_r.at[in_half])
-    in_wout = load(coarse_out, wout, load_sem.at[5])
-    in_wup = load(up_weight, wup, load_sem.at[6])
-    for peer in peers:
-        pl.semaphore_signal(barrier, inc=1, device_id=peer, device_id_type=pl.DeviceIdType.MESH)
     pl.semaphore_wait(barrier, len(peers))
+    in_wout = load(coarse_out, wout, load_sem.at[6])
+    in_wup = load(up_weight, wup, load_sem.at[7])
 
     sent = []
     halo = remote(tokens, both.at[pl.ds(0, rows)], halo_s, halo_r, linear(after))
@@ -285,7 +301,7 @@
     def send_qk(offsets):
         for d in offsets:
             dest = toggle(me_s, d)
-            for k, source in enumerate((coarse_query, coarse_kv.at[0])):
+            for k, source in enumerate((coarse_query, kv.at[0])):
                 sent.append(
                     remote(
                         source.at[:, head_cols(dest)], wqk.at[block_of(me_s), pl.ds(k * own, own)],
@@ -299,7 +315,7 @@
             for k, head in enumerate((flip(dest, half), dest)):
                 sent.append(
                     remote(
-                        coarse_kv.at[1, :, head_cols(head)],
+                        kv.at[1, :, head_cols(head)],
                         wv.at[block_of(in_half), pl.ds(k * own, own)],
                         v_s.at[2 * (d - 1) + k], v_r.at[in_half], {"seq": dest},
                     )
@@ -395,23 +411,26 @@
     project_rows(0)
     issue(2)
 
-    row_index = lax.broadcasted_iota(jnp.int32, (rows, 2 * rows), 0)
-    col_index = lax.broadcasted_iota(jnp.int32, (rows, 2 * rows), 1)
-    offset = row_index + rows - col_index
-    allowed = (offset >= 0) & (offset < WINDOW) & (lin * rows - rows + col_index >= 0)
-
-    def weigh(query, key, mask):
-        scores = jnp.where(mask, dot_t(query, key) * scale, big_negative)
-        peak = jnp.max(scores, axis=-1, keepdims=True)
-        weights = jnp.where(mask, jnp.exp(scores - peak), 0.0)
-        return weights.astype(bf), jnp.sum(weights, axis=-1, keepdims=True)
-
-    @pl.loop(0, width // HEAD)
+    own_side = lax.broadcasted_iota(jnp.int32, (rows, rows), 1) <= lax.broadcasted_iota(
+        jnp.int32, (rows, rows), 0
+    )
+    bias = jnp.where(lin > 0, 0.0, big_negative)
+
+    @pl.loop(0, width // HEAD, unroll=4)
     def _(h):
         cols = pl.ds(pl.multiple_of(h * HEAD, HEAD), HEAD)
         vcols = pl.ds(pl.multiple_of(width + h * HEAD, HEAD), HEAD)
-        weights, denom = weigh(queries[:, cols], key_rows[:, cols], allowed)
-        local[:, cols] = (dot32(weights, key_rows[:, vcols]) / denom).astype(bf)
+        query = queries[:, cols]
+        late = dot_t(query, key_rows[rows:, cols])
+        early = dot_t(query, key_rows[:rows, cols]) + bias
+        scores = jnp.where(own_side, late, early) * scale
+        peak = jnp.max(scores, axis=-1, keepdims=True)
+        weights = jnp.exp(scores - peak)
+        denom = jnp.sum(weights, axis=-1, keepdims=True)
+        late = jnp.where(own_side, weights, 0.0).astype(bf)
+        early = jnp.where(own_side, 0.0, weights).astype(bf)
+        out = dot32(late, key_rows[rows:, vcols]) + dot32(early, key_rows[:rows, vcols])
+        local[:, cols] = (out / denom).astype(bf)
 
     in_wo.wait()
 
@@ -470,33 +489,28 @@
     for d in range(1, tp):
         slot = ss_tp.at[me_t]
         group.append(remote(slot, slot, ssa_s.at[d - 1], ssa_r.at[d - 1], {"tp": toggle(me_t, d)}))
-    evens = sorted(range(2, seq, 2), key=lambda m: (bin(m).count("1"), m))
-    for at, mask in enumerate(evens):
-        gather[mask].wait_recv()
-        spread_block(mask)
-        issue(5 + at)
-
-    for piece in range(pieces):
-        forward_down(piece)
-    for copy in group:
-        copy.wait_recv()
-    sent.extend(group)
-    whole_sum = ss_tp[0]
-    for t in range(1, tp):
-        whole_sum += ss_tp[t]
-    ss_seq[me_s] = whole_sum
+    issue(5)
     ss_copies = []
-    for d in range(1, seq):
-        slot = ss_seq.at[me_s]
-        ss_copies.append(
-            remote(slot, slot, ssb_s.at[d - 1], ssb_r.at[d - 1], {"seq": toggle(me_s, d)})
-        )
-    sent.extend(ss_copies)
-    for hs in range(half):
-        arrived(wv.at[pl.ds(hs * depth, depth)], v_r.at[hs])
+
+    def gather_sums():
+        for copy in group:
+            copy.wait_recv()
+        sent.extend(group)
+        whole_sum = ss_tp[0]
+        for t in range(1, tp):
+            whole_sum += ss_tp[t]
+        ss_seq[me_s] = whole_sum
+        for d in range(1, seq):
+            slot = ss_seq.at[me_s]
+            ss_copies.append(
+                remote(slot, slot, ssb_s.at[d - 1], ssb_r.at[d - 1], {"seq": toggle(me_s, d)})
+            )
+        sent.extend(ss_copies)
+
     half_cols = pl.ds(pl.multiple_of(zh * half * depth, half * depth), half * depth)
     pv_copies = []
-    for piece in range(pieces):
+
+    def v_piece(piece):
         finish_down(piece)
         at = slice(piece * span, (piece + 1) * span)
         product = dot32(down_g[at, half_cols], wv[...])
@@ -506,6 +520,24 @@
         pv_copies.append(
             remote(pv_out.at[at], pv_in.at[at], pv_s.at[piece], pv_r.at[piece], {"seq": partner})
         )
+
+    evens = sorted(range(2, seq, 2), key=lambda m: (bin(m).count("1"), m))
+    for at, mask in enumerate(evens):
+        gather[mask].wait_recv()
+        spread_block(mask)
+        if at == max(0, len(evens) - 2):
+            gather_sums()
+        issue(6 + at)
+        if at == max(0, len(evens) - 2):
+            for hs in range(half):
+                arrived(wv.at[pl.ds(hs * depth, depth)], v_r.at[hs])
+            for piece in range(pieces // 2):
+                forward_down(piece)
+            for piece in range(pieces // 2):
+                v_piece(piece)
+    for piece in range(pieces // 2, pieces):
+        forward_down(piece)
+        v_piece(piece)
     sent.extend(pv_copies)
     for mask in range(1, seq, 2):
         gather[mask].wait_recv()
@@ -520,14 +552,6 @@
         copy.wait_recv()
     sent.extend(pending)
 
-    for source in range(seq):
-        arrived(wqk.at[pl.ds(source * depth, depth)], qk_r.at[source])
-
-    @pl.loop(0, pieces)
-    def _(i):
-        at = pl.ds(pl.multiple_of(i * span, span), span)
-        mixed_qk[at, :] = dot32(down_g[at, :], wqk[...]).astype(bf)
-
     for copy in ss_copies:
         copy.wait_recv()
     sums = jnp.concatenate([ss_seq[s, 0:1, :] for s in range(seq)], 0)
@@ -537,20 +561,6 @@
         factors[s * crows : (s + 1) * crows, :] = jnp.broadcast_to(
             turned[:, s : s + 1], (crows, HEAD)
         )
-    block = 2 * crows
-
-    def project(columns, mixed):
-        @pl.loop(0, seq // 2)
-        def _(i):
-            at = pl.ds(pl.multiple_of(i * block, block), block)
-            pooled = pooled_all[pl.ds(i * 2 * tp, 2 * tp)].reshape(block, width)
-            product = dot32(pooled, mixed[...])
-            for c in range(product.shape[1] // HEAD):
-                part = product[:, c * HEAD : (c + 1) * HEAD] * factors[at, :]
-                first = columns + c * HEAD
-                qkv[at, first : first + HEAD] = part.astype(bf)
-
-    project(0, mixed_qk)
 
     earlier = pooled_all[before_slot(me_s, tp, total), pool_rows - 16 :, :]
     for u in range(2):
@@ -561,6 +571,31 @@
         top = lax.broadcasted_iota(jnp.int32, rolled.shape, 0) == 0
         short_cols[pl.ds(0, crows), cols] = jnp.where(top, last, rolled)
 
+    for source in range(seq):
+        arrived(wqk.at[pl.ds(source * depth, depth)], qk_r.at[source])
+
+    @pl.loop(0, pieces)
+    def _(i):
+        at = pl.ds(pl.multiple_of(i * span, span), span)
+        mixed_qk[at, :] = dot32(down_g[at, :], wqk[...]).astype(bf)
+
+    block = 2 * crows
+
+    def project(columns, mixed):
+        @pl.loop(0, seq // 2)
+        def _(i):
+            at = pl.ds(pl.multiple_of(i * block, block), block)
+            pooled = pooled_all[pl.ds(i * 2 * tp, 2 * tp)].reshape(block, width)
+            product = dot32(pooled, mixed[...])
+            for c in range(product.shape[1] // HEAD):
+                first = columns + c * HEAD
+                part = product[:, c * HEAD : (c + 1) * HEAD] * factors[at, :]
+                if first < own:
+                    part = part * scale
+                qkv[at, first : first + HEAD] = part.astype(bf)
+
+    project(0, mixed_qk)
+
     for copy in pv_copies:
         copy.wait_recv()
     mixed_v[...] = (mv[...] + pv_in[...].astype(f32)).astype(bf)
@@ -573,16 +608,29 @@
             recv_sem=h_r.at[me_s], device_id={"seq": index}, device_id_type=pl.DeviceIdType.MESH,
         )
 
+    r = lax.broadcasted_iota(jnp.int32, (block, block), 0)
+    causal = lax.broadcasted_iota(jnp.int32, (block, block), 1) <= r
     for i in range(seq // 2):
         extent = (i + 1) * block
-        r = lax.broadcasted_iota(jnp.int32, (block, extent), 0) + i * block
-        c = lax.broadcasted_iota(jnp.int32, (block, extent), 1)
+        start = i * block
         for h in range(own // HEAD):
             part = slice(h * HEAD, (h + 1) * HEAD)
             kpart = slice(own + h * HEAD, own + (h + 1) * HEAD)
             vpart = slice(2 * own + h * HEAD, 2 * own + (h + 1) * HEAD)
-            weights, denom = weigh(qkv[i * block : extent, part], qkv[:extent, kpart], c <= r)
-            out = dot32(weights, qkv[:extent, vpart]) / denom
+            query = qkv[start:extent, part]
+            near = jnp.where(causal, dot_t(query, qkv[start:extent, kpart]), big_negative)
+            peak = jnp.max(near, axis=-1, keepdims=True)
+            if i:
+                far = dot_t(query, qkv[:start, kpart])
+                peak = jnp.maximum(peak, jnp.max(far, axis=-1, keepdims=True))
+            weights = jnp.exp(near - peak)
+            denom = jnp.sum(weights, axis=-1, keepdims=True)
+            out = dot32(weights.astype(bf), qkv[start:extent, vpart])
+            if i:
+                weights = jnp.exp(far - peak)
+                denom += jnp.sum(weights, axis=-1, keepdims=True)
+                out += dot32(weights.astype(bf), qkv[:start, vpart])
+            out = out / denom
             shifted[i * block + 1 : extent + 1, part] = out
         for index in (2 * i, 2 * i + 1):
             heads_out[index] = shifted[index * crows : (index + 1) * crows, :].astype(bf)
@@ -726,6 +774,7 @@
                   anywhere, anywhere, anywhere],
         out_specs=vmem,
         scratch_shapes=[
+            V(coarse_keyval.shape, bf), V((2, depth, local_cols), bf),
             V((2 * rows, width), bf), V(fine_query.shape, bf), V(fine_keyval.shape, bf),
             V(fine_out.shape, bf), V(down_weight.shape, bf), V((width, seq * depth), bf),
             V((seq * depth, 2 * own), bf), V((half * depth, 2 * own), bf),
@@ -741,7 +790,7 @@
             V((tp - 1, crows, local_cols), bf), V((tp - 1, crows, local_cols), bf),
             V((crows, local_cols), bf),
             V((2 * (tp - 1), pool_rows, width // 2), bf), V((2 * (tp - 1), pool_rows, width // 2), bf),
-            dma(7), one(()), one(()), dma(2 * (seq - 1)), dma(seq), dma(2 * (half - 1)), dma(half),
+            dma(8), one(()), one(()), dma(2 * (seq - 1)), dma(seq), dma(2 * (half - 1)), dma(half),
             dma(4 * (tp - 1)), dma(4 * (tp - 1)), dma(tp - 1), dma(tp - 1),
             dma(seq - 1), dma(seq - 1), dma(seq - 1), dma(seq - 1),
             dma(tp - 1), dma(tp - 1), dma(seq - 1), dma(seq - 1), dma(4), dma(4),
@@ -752,7 +801,7 @@
             collective_id=0, has_side_effects=True, vmem_limit_bytes=62 * 1024 * 1024
         ),
     )(tokens, fine_gain[None], fine_query, fine_keyval, fine_out, down_weight, coarse_gain[None],
-      coarse_query, jnp.transpose(coarse_keyval, (1, 0, 2)), coarse_out, up_weight)
+      coarse_query, coarse_keyval, coarse_out, up_weight)
 
 
 def chosen(*args):

time: 106 us -> 105 us (level); the launches traced: 105 us -> 103 us
  local copies, waits for them, and re-layouts: 5.43 us -> 1.87 us
    unnamed x2 -> x1, local copies, waits for them, and re-layouts: 5.43 us -> 1.87 us
    pallas_call x1, Pallas kernels: 100 us -> 101 us  [head_body(): pl.pallas_call(functools.partial(section_kernel, seq, tp), out_shape=jax....]
where the time goes in v4:
time: 105 us; the launch traced here: 103 us
  Pallas kernels  101 us (96%)
  local copies, waits for them, and re-layouts  1.87 us (2%)
    pallas_call x1, Pallas kernels, head_body(): pl.pallas_call(functools.partial(section_kernel, seq, tp), out_shape=jax....  101 us

profile of v4, /device:TPU:19, one launch (start us, length us, event | category | flops | bytes accessed | tf_op | source)
XLA Modules:
  0.0 103.0 jit_solution(2481271638992466477)
XLA Ops:
  0.0 101.1 %shard_map.109 = bf16[256,1024]{1,0:T(8,128)(2,1)} custom-call(bf16[256,1024]{1,0:T(8,128)(2,1)} %tokens.1, f32[1,1024]{1,0:T(1,128)} %bitcast.3, bf16[1024,1024]{1,0:T(8,128)(2,1)} %fine_query.1, bf16[1024,2048]{1,0:T(8,128)(2,1)} %fine_keyval.1, bf16[1024,1024]{1,0:T(8,128)(2,1)} %fine_out.1, bf16[1024,1024]{1,0:T(8,128)(2,1)} %down_weight.1, ...), custom_call_target="tpu_custom_call" | custom-call | tf_op jit(solution)/shard_map/pallas_call | solution.py:770
  101.1 1.9 %copy.13 = bf16[256,1024]{1,0:T(8,128)(2,1)} copy(bf16[256,1024]{1,0:T(8,128)(2,1)} %shard_map.109) | data formatting | bytes 1048576

commit v5 on v4

--- a/solution.py
+++ b/solution.py
@@ -176,15 +176,17 @@
     )
 
 
+END_ORDER = (4, 6, 1, 5, 2, 7, 3)
+INNER_ORDER = (4, 6, 1, 5, 2, 7, 3)
 PLAN = (
-    (("down", 0), ("qk", 4)),
-    (("v", 3), ("v", 1), ("v", 2), ("qk", 6), ("qk", 1)),
+    (("down", 0), ("qk", 1)),
+    (("v", 3), ("v", 1), ("v", 2), ("qk", 2), ("qk", 3)),
     (),
     (("down", 1),),
-    (("qk", 5), ("qk", 2)),
+    (("qk", 4), ("qk", 5)),
     (("down", 2),),
     (("down", 3),),
-    (("qk", 7), ("qk", 3)),
+    (("qk", 6), ("qk", 7)),
     (),
 )
 
@@ -194,7 +196,7 @@
     tokens, fine_gain, fine_query, fine_keyval, fine_out, down_weight, coarse_gain, coarse_query,
     coarse_kv, coarse_out, up_weight,
     result,
-    kv_raw, kv, both, wq, wkv, wo, down_own, down_g, wqk, wv, wout, wup,
+    fgain, cgains, kv_raw, kv, both, wq, wkv, wo, down_own, down_g, wqk, wv, wout, wup,
     normed, queries, key_rows, local, fine_state, pooled_all, mv, pv_out, pv_in, mixed_qk,
     mixed_v, qkv, factors, shifted, heads_out, heads_in, coarse_heads, short_cols, lift,
     ss_tp, ss_seq, send1, recv1, state, send2, recv2,
@@ -265,6 +267,8 @@
     peers += [linear(after), linear(before)]
     in_kv = load(coarse_kv, kv_raw, load_sem.at[5])
     in_down = load(down_weight, down_own, load_sem.at[4])
+    in_cgain = load(coarse_gain, cgains, load_sem.at[8])
+    in_fgain = load(fine_gain, fgain, load_sem.at[9])
     in_tokens = load(tokens, both.at[pl.ds(rows, rows)], load_sem.at[0])
     load(coarse_query.at[:, head_cols(me_s)], wqk.at[block_of(me_s), pl.ds(0, own)], qk_r.at[me_s])
     for peer in peers:
@@ -298,14 +302,19 @@
     sent = []
     halo = remote(tokens, both.at[pl.ds(0, rows)], halo_s, halo_r, linear(after))
 
-    def send_qk(offsets):
-        for d in offsets:
-            dest = toggle(me_s, d)
+    inner = lax.rem(lax.div(me_s, half) + lax.div(me_s, max(half // 2, 1)), 2)
+
+    def send_qk(slots):
+        for n in slots:
+            dest = toggle(me_s, n)
+            if seq == len(END_ORDER) + 1:
+                dest = toggle(me_s, END_ORDER[n - 1])
+                dest += inner * (toggle(me_s, INNER_ORDER[n - 1]) - dest)
             for k, source in enumerate((coarse_query, kv.at[0])):
                 sent.append(
                     remote(
                         source.at[:, head_cols(dest)], wqk.at[block_of(me_s), pl.ds(k * own, own)],
-                        qk_s.at[2 * (d - 1) + k], qk_r.at[me_s], {"seq": dest},
+                        qk_s.at[2 * (n - 1) + k], qk_r.at[me_s], {"seq": dest},
                     )
                 )
 
@@ -325,7 +334,8 @@
     pieces = 4
     span = width // pieces
     in_down.wait()
-    cgain = coarse_gain[:, pl.ds(pl.multiple_of(me_t * fcols, fcols), fcols)]
+    in_cgain.wait()
+    cgain = cgains[:, pl.ds(pl.multiple_of(me_t * fcols, fcols), fcols)]
 
     def slot_cols(slot):
         return pl.ds(pl.multiple_of(slot * fcols, fcols), fcols)
@@ -378,7 +388,8 @@
 
     issue(0)
 
-    gain = fine_gain[...]
+    in_fgain.wait()
+    gain = fgain[...]
 
     def norm_rows(first):
         values = both[pl.ds(first, rows), :].astype(f32)
@@ -770,10 +781,10 @@
     return pl.pallas_call(
         functools.partial(section_kernel, seq, tp),
         out_shape=jax.ShapeDtypeStruct((rows, width), bf),
-        in_specs=[anywhere, vmem, anywhere, anywhere, anywhere, anywhere, vmem, anywhere,
-                  anywhere, anywhere, anywhere],
+        in_specs=[anywhere] * 11,
         out_specs=vmem,
         scratch_shapes=[
+            V((1, width), f32), V((1, tp * local_cols), f32),
             V(coarse_keyval.shape, bf), V((2, depth, local_cols), bf),
             V((2 * rows, width), bf), V(fine_query.shape, bf), V(fine_keyval.shape, bf),
             V(fine_out.shape, bf), V(down_weight.shape, bf), V((width, seq * depth), bf),
@@ -790,7 +801,7 @@
             V((tp - 1, crows, local_cols), bf), V((tp - 1, crows, local_cols), bf),
             V((crows, local_cols), bf),
             V((2 * (tp - 1), pool_rows, width // 2), bf), V((2 * (tp - 1), pool_rows, width // 2), bf),
-            dma(8), one(()), one(()), dma(2 * (seq - 1)), dma(seq), dma(2 * (half - 1)), dma(half),
+            dma(10), one(()), one(()), dma(2 * (seq - 1)), dma(seq), dma(2 * (half - 1)), dma(half),
             dma(4 * (tp - 1)), dma(4 * (tp - 1)), dma(tp - 1), dma(tp - 1),
             dma(seq - 1), dma(seq - 1), dma(seq - 1), dma(seq - 1),
             dma(tp - 1), dma(tp - 1), dma(seq - 1), dma(seq - 1), dma(4), dma(4),
@@ -798,10 +809,11 @@
             dma(2 * (tp - 1)),
         ],
         compiler_params=pltpu.CompilerParams(
-            collective_id=0, has_side_effects=True, vmem_limit_bytes=62 * 1024 * 1024
+            collective_id=0, has_side_effects=True, vmem_limit_bytes=54000 * 1024
         ),
-    )(tokens, fine_gain[None], fine_query, fine_keyval, fine_out, down_weight, coarse_gain[None],
-      coarse_query, coarse_keyval, coarse_out, up_weight)
+    )(*(pltpu.with_memory_space_constraint(x, pltpu.HBM) for x in (
+        tokens, fine_gain[None], fine_query, fine_keyval, fine_out, down_weight, coarse_gain[None],
+        coarse_query, coarse_keyval, coarse_out, up_weight)))
 
 
 def chosen(*args):

time: 105 us -> 102 us (0.971)
  Pallas kernels: 101 us -> 99.7 us
  local copies, waits for them, and re-layouts: 1.87 us -> 0.8 us
    pallas_call x1, Pallas kernels: 101 us -> 99.7 us  [head_body(): pl.pallas_call(functools.partial(section_kernel, seq, tp), out_shape=jax....]
    unnamed x1, local copies, waits for them, and re-layouts: 1.87 us -> 0.8 us
where the time goes in v5:
time: 102 us; the launch traced here: 101 us
  Pallas kernels  99.7 us (98%)
    pallas_call x1, Pallas kernels, head_body(): pl.pallas_call(functools.partial(section_kernel, seq, tp), out_shape=jax....  99.7 us

profile of v5, /device:TPU:19, one launch (start us, length us, event | category | flops | bytes accessed | tf_op | source)
XLA Modules:
  0.0 100.5 jit_solution(13707566331313172899)
XLA Ops:
  0.0 99.7 %shard_map.109 = bf16[256,1024]{1,0:T(8,128)(2,1)S(1)} custom-call(bf16[256,1024]{1,0:T(8,128)(2,1)} %tokens.1, f32[1,1024]{1,0:T(1,128)} %bitcast.3, bf16[1024,1024]{1,0:T(8,128)(2,1)} %fine_query.1, bf16[1024,2048]{1,0:T(8,128)(2,1)} %fine_keyval.1, bf16[1024,1024]{1,0:T(8,128)(2,1)} %fine_out.1, bf16[1024,1024]{1,0:T(8,128)(2,1)} %down_weight.1, ...), custom_call_target="tpu_custom_call" | custom-call | tf_op jit(solution)/shard_map/pallas_call | solution.py:781
  99.7 0.8 copy.13

commit v6 on v5

--- a/solution.py
+++ b/solution.py
@@ -176,17 +176,17 @@
     )
 
 
-END_ORDER = (4, 6, 1, 5, 2, 7, 3)
-INNER_ORDER = (4, 6, 1, 5, 2, 7, 3)
+END_ORDER = (1, 2, 3, 4, 5, 6, 7)
+INNER_ORDER = (1, 2, 3, 4, 5, 6, 7)
 PLAN = (
-    (("down", 0), ("qk", 1)),
-    (("v", 3), ("v", 1), ("v", 2), ("qk", 2), ("qk", 3)),
+    (("down", 0), ("qk", 4)),
+    (("v", 3), ("v", 1), ("v", 2), ("qk", 6), ("qk", 1)),
     (),
     (("down", 1),),
-    (("qk", 4), ("qk", 5)),
+    (("qk", 5),),
     (("down", 2),),
-    (("down", 3),),
-    (("qk", 6), ("qk", 7)),
+    (("qk", 7), ("down", 3)),
+    (("qk", 2), ("qk", 3)),
     (),
 )
 
@@ -197,8 +197,8 @@
     coarse_kv, coarse_out, up_weight,
     result,
     fgain, cgains, kv_raw, kv, both, wq, wkv, wo, down_own, down_g, wqk, wv, wout, wup,
-    normed, queries, key_rows, local, fine_state, pooled_all, mv, pv_out, pv_in, mixed_qk,
-    mixed_v, qkv, factors, shifted, heads_out, heads_in, coarse_heads, short_cols, lift,
+    normed, queries, key_rows, local, fine_state, pooled_all, mqk, mv, pv_out, pv_in, mixed_qk,
+    mixed_v, qkv, factors, shifted, heads_out, coarse_heads, short_cols, lift,
     ss_tp, ss_seq, send1, recv1, state, send2, recv2,
     load_sem, halo_s, halo_r, qk_s, qk_r, v_s, v_r, d_s, d_r, pa_s, pa_r, pb_s, pb_r, pc_s, pc_r,
     ssa_s, ssa_r, ssb_s, ssb_r, pv_s, pv_r, h_s, h_r, r1_s, r1_r, r2_s, r2_r,
@@ -550,6 +550,27 @@
         forward_down(piece)
         v_piece(piece)
     sent.extend(pv_copies)
+    def add_pair(pair, first, last):
+        for j in range(2):
+            arrived(wqk.at[block_of(2 * pair + j)], qk_r.at[2 * pair + j])
+        both_rows = pl.ds(pl.multiple_of(2 * depth * pair, 2 * depth), 2 * depth)
+
+        @pl.loop(0, pieces)
+        def _(i):
+            at = pl.ds(pl.multiple_of(i * span, span), span)
+            product = dot32(down_g[at, both_rows], wqk[both_rows, :])
+            if not first:
+                product += mqk[at, :]
+            if last:
+                mixed_qk[at, :] = product.astype(bf)
+            else:
+                mqk[at, :] = product
+
+    pair_masks = [0] + [m for m in range(half - 1, 1, -1)][::-1] + [1]
+    pairs = [toggle(lax.div(me_s, 2), mask) for mask in pair_masks]
+    for n, pair in enumerate(pairs[: half // 2]):
+        add_pair(pair, n == 0, False)
+
     for mask in range(1, seq, 2):
         gather[mask].wait_recv()
     sent.extend(gather.values())
@@ -559,6 +580,8 @@
         pending.append(
             remote(part, part, pc_s.at[k], pc_r.at[k], {"tp": flip(me_t, core_bit)})
         )
+    for pair in pairs[half // 2 : -1]:
+        add_pair(pair, False, False)
     for copy in pending:
         copy.wait_recv()
     sent.extend(pending)
@@ -582,14 +605,7 @@
         top = lax.broadcasted_iota(jnp.int32, rolled.shape, 0) == 0
         short_cols[pl.ds(0, crows), cols] = jnp.where(top, last, rolled)
 
-    for source in range(seq):
-        arrived(wqk.at[pl.ds(source * depth, depth)], qk_r.at[source])
-
-    @pl.loop(0, pieces)
-    def _(i):
-        at = pl.ds(pl.multiple_of(i * span, span), span)
-        mixed_qk[at, :] = dot32(down_g[at, :], wqk[...]).astype(bf)
-
+    add_pair(pairs[-1], False, True)
     block = 2 * crows
 
     def project(columns, mixed):
@@ -615,7 +631,7 @@
 
     def heads_copy(index):
         return pltpu.make_async_remote_copy(
-            src_ref=heads_out.at[index], dst_ref=heads_in.at[me_s], send_sem=h_s.at[index],
+            src_ref=heads_out.at[index], dst_ref=coarse_heads.at[:, head_cols(me_s)], send_sem=h_s.at[index],
             recv_sem=h_r.at[me_s], device_id={"seq": index}, device_id_type=pl.DeviceIdType.MESH,
         )
 
@@ -650,18 +666,16 @@
             def _(index=index):
                 heads_copy(index).start()
 
-    heads_in[me_s] = heads_out[me_s]
+    coarse_heads[:, head_cols(me_s)] = heads_out[me_s]
     in_wout.wait()
     in_wup.wait()
     for j in range(seq):
 
         @pl.when(me_s != j)
         def _(j=j):
-            arrived(heads_in.at[j], h_r.at[j])
-
-        coarse_heads[:, j * own : (j + 1) * own] = heads_in[j]
-
-    sides = 2
+            arrived(coarse_heads.at[:, pl.ds(j * own, own)], h_r.at[j])
+
+    sides, ways = 4, 2
     side = fcols // sides
 
     def partial(t, u, store):
@@ -709,8 +723,8 @@
             whole += recv1[bit - 1, :, ucols].astype(f32)
         top = lax.broadcasted_iota(jnp.int32, whole.shape, 0) == 0
         state[:, ucols] = jnp.where(top & (me_s == 0), 0.0, whole).astype(bf)
-        for w in range(sides):
-            wcols = slice(w * width // sides, (w + 1) * width // sides)
+        for w in range(ways):
+            wcols = slice(w * width // ways, (w + 1) * width // ways)
             product = dot32(state[:, ucols], wup[ucols, wcols])
             if u:
                 product += lift[:, wcols]
@@ -719,7 +733,7 @@
                 for d in tp_order:
                     dest = around(me_t, d, tp)
                     some = pl.ds(pl.multiple_of(dest * pool_rows, pool_rows), pool_rows)
-                    at = (d - 1) * sides + w
+                    at = (d - 1) * ways + w
                     send2[at] = lift[some, wcols].astype(bf)
                     r2.append(
                         remote(
@@ -727,15 +741,15 @@
                         )
                     )
     sent.extend(r2)
-    for w in range(sides):
-        wcols = slice(w * width // sides, (w + 1) * width // sides)
+    for w in range(ways):
+        wcols = slice(w * width // ways, (w + 1) * width // ways)
         for copy in r2[w * (tp - 1) : (w + 1) * (tp - 1)]:
             copy.wait_recv()
         lifted = lift[pl.ds(pl.multiple_of(me_t * pool_rows, pool_rows), pool_rows), wcols]
         for d in range(1, tp):
-            lifted += recv2[(d - 1) * sides + w].astype(f32)
-        spread = jnp.broadcast_to(lifted[:, None, :], (pool_rows, SHORT, width // sides))
-        spread = spread.reshape(rows, width // sides)
+            lifted += recv2[(d - 1) * ways + w].astype(f32)
+        spread = jnp.broadcast_to(lifted[:, None, :], (pool_rows, SHORT, width // ways))
+        spread = spread.reshape(rows, width // ways)
         result[:, wcols] = (fine_state[:, wcols].astype(f32) + spread).astype(bf)
     for index in range(seq):
 
@@ -792,10 +806,10 @@
             V(coarse_out.shape, bf), V(up_weight.shape, bf),
             V((2 * rows, width), bf), V((rows, width), bf), V((2 * rows, 2 * width), bf),
             V((rows, width), bf), V((rows, width), bf), V((seq * tp, pool_rows, width), bf),
-            V((width, own), f32), V((width, own), bf),
+            V((width, 2 * own), f32), V((width, own), f32), V((width, own), bf),
             V((width, own), bf), V((width, 2 * own), bf), V((width, own), bf),
             V((count, 3 * own), bf), V((count, HEAD), f32),
-            V((count + 8, own), f32), V((seq, crows, own), bf), V((seq, crows, own), bf),
+            V((count + 8, own), f32), V((seq, crows, own), bf),
             V((crows, local_cols), bf), V((crows, local_cols), f32), V((crows, width), f32),
             V((tp, 8, crows), f32), V((seq, 8, crows), f32),
             V((tp - 1, crows, local_cols), bf), V((tp - 1, crows, local_cols), bf),
@@ -805,7 +819,7 @@
             dma(4 * (tp - 1)), dma(4 * (tp - 1)), dma(tp - 1), dma(tp - 1),
             dma(seq - 1), dma(seq - 1), dma(seq - 1), dma(seq - 1),
             dma(tp - 1), dma(tp - 1), dma(seq - 1), dma(seq - 1), dma(4), dma(4),
-            dma(seq), dma(seq), dma(2 * (tp - 1)), dma(2 * (tp - 1)), dma(2 * (tp - 1)),
+            dma(seq), dma(seq), dma(4 * (tp - 1)), dma(4 * (tp - 1)), dma(2 * (tp - 1)),
             dma(2 * (tp - 1)),
         ],
         compiler_params=pltpu.CompilerParams(

time: 102 us -> 101 us (level)
  no operation moved by 1% of the time
where the time goes in v6:
time: 101 us; the launch traced here: 100 us
  Pallas kernels  99.6 us (99%)
    pallas_call x1, Pallas kernels, head_body(): pl.pallas_call(functools.partial(section_kernel, seq, tp), out_shape=jax....  99.6 us

profile of v6, /device:TPU:19, one launch (start us, length us, event | category | flops | bytes accessed | tf_op | source)
XLA Modules:
  0.0 100.4 jit_solution(446899218911695510)
XLA Ops:
  0.0 99.6 %shard_map.109 = bf16[256,1024]{1,0:T(8,128)(2,1)S(1)} custom-call(bf16[256,1024]{1,0:T(8,128)(2,1)} %tokens.1, f32[1,1024]{1,0:T(1,128)} %bitcast.3, bf16[1024,1024]{1,0:T(8,128)(2,1)} %fine_query.1, bf16[1024,2048]{1,0:T(8,128)(2,1)} %fine_keyval.1, bf16[1024,1024]{1,0:T(8,128)(2,1)} %fine_out.1, bf16[1024,1024]{1,0:T(8,128)(2,1)} %down_weight.1, ...), custom_call_target="tpu_custom_call" | custom-call | tf_op jit(solution)/shard_map/pallas_call | solution.py:795
  99.6 0.8 copy.13

commit v7 on v6

--- a/solution.py
+++ b/solution.py
@@ -176,16 +176,14 @@
     )
 
 
-END_ORDER = (1, 2, 3, 4, 5, 6, 7)
-INNER_ORDER = (1, 2, 3, 4, 5, 6, 7)
 PLAN = (
     (("down", 0), ("qk", 4)),
     (("v", 3), ("v", 1), ("v", 2), ("qk", 6), ("qk", 1)),
     (),
     (("down", 1),),
-    (("qk", 5),),
+    (("qk", 7),),
     (("down", 2),),
-    (("qk", 7), ("down", 3)),
+    (("qk", 5), ("down", 3)),
     (("qk", 2), ("qk", 3)),
     (),
 )
@@ -302,14 +300,9 @@
     sent = []
     halo = remote(tokens, both.at[pl.ds(0, rows)], halo_s, halo_r, linear(after))
 
-    inner = lax.rem(lax.div(me_s, half) + lax.div(me_s, max(half // 2, 1)), 2)
-
-    def send_qk(slots):
-        for n in slots:
+    def send_qk(offsets):
+        for n in offsets:
             dest = toggle(me_s, n)
-            if seq == len(END_ORDER) + 1:
-                dest = toggle(me_s, END_ORDER[n - 1])
-                dest += inner * (toggle(me_s, INNER_ORDER[n - 1]) - dest)
             for k, source in enumerate((coarse_query, kv.at[0])):
                 sent.append(
                     remote(
@@ -538,7 +531,6 @@
         spread_block(mask)
         if at == max(0, len(evens) - 2):
             gather_sums()
-        issue(6 + at)
         if at == max(0, len(evens) - 2):
             for hs in range(half):
                 arrived(wv.at[pl.ds(hs * depth, depth)], v_r.at[hs])
@@ -546,6 +538,7 @@
                 forward_down(piece)
             for piece in range(pieces // 2):
                 v_piece(piece)
+        issue(6 + at)
     for piece in range(pieces // 2, pieces):
         forward_down(piece)
         v_piece(piece)
@@ -566,7 +559,7 @@
             else:
                 mqk[at, :] = product
 
-    pair_masks = [0] + [m for m in range(half - 1, 1, -1)][::-1] + [1]
+    pair_masks = [0] + list(range(half - 1, 1, -1)) + [1]
     pairs = [toggle(lax.div(me_s, 2), mask) for mask in pair_masks]
     for n, pair in enumerate(pairs[: half // 2]):
         add_pair(pair, n == 0, False)

time: 101 us -> 99.3 us (0.983)
  Pallas kernels: 99.6 us -> 97.8 us
    pallas_call x1, Pallas kernels: 99.6 us -> 97.8 us  [head_body(): pl.pallas_call(functools.partial(section_kernel, seq, tp), out_shape=jax....]
where the time goes in v7:
time: 99.3 us; the launch traced here: 98.6 us
  Pallas kernels  97.8 us (98%)
    pallas_call x1, Pallas kernels, head_body(): pl.pallas_call(functools.partial(section_kernel, seq, tp), out_shape=jax....  97.8 us

profile of v7, /device:TPU:19, one launch (start us, length us, event | category | flops | bytes accessed | tf_op | source)
XLA Modules:
  0.0 98.6 jit_solution(326041929444928059)
XLA Ops:
  0.0 97.8 %shard_map.109 = bf16[256,1024]{1,0:T(8,128)(2,1)S(1)} custom-call(bf16[256,1024]{1,0:T(8,128)(2,1)} %tokens.1, f32[1,1024]{1,0:T(1,128)} %bitcast.3, bf16[1024,1024]{1,0:T(8,128)(2,1)} %fine_query.1, bf16[1024,2048]{1,0:T(8,128)(2,1)} %fine_keyval.1, bf16[1024,1024]{1,0:T(8,128)(2,1)} %fine_out.1, bf16[1024,1024]{1,0:T(8,128)(2,1)} %down_weight.1, ...), custom_call_target="tpu_custom_call" | custom-call | tf_op jit(solution)/shard_map/pallas_call | solution.py:788
  97.9 0.8 copy.13

commit v8 on v7

--- a/solution.py
+++ b/solution.py
@@ -177,7 +177,7 @@
 
 
 PLAN = (
-    (("down", 0), ("qk", 4)),
+    (("qk", 4),),
     (("v", 3), ("v", 1), ("v", 2), ("qk", 6), ("qk", 1)),
     (),
     (("down", 1),),
@@ -271,32 +271,7 @@
     load(coarse_query.at[:, head_cols(me_s)], wqk.at[block_of(me_s), pl.ds(0, own)], qk_r.at[me_s])
     for peer in peers:
         pl.semaphore_signal(barrier, inc=1, device_id=peer, device_id_type=pl.DeviceIdType.MESH)
-    in_kv.wait()
-    in_wq = load(fine_query, wq, load_sem.at[2])
-    in_wkv = load(fine_keyval, wkv, load_sem.at[1])
-    in_wo = load(fine_out, wo, load_sem.at[3])
-    step = HEAD
-    picks = []
-    for k in range(2):
-        r = lax.broadcasted_iota(jnp.int32, (step, 2 * step), 0)
-        c = lax.broadcasted_iota(jnp.int32, (step, 2 * step), 1)
-        picks.append((c == 2 * r + k).astype(bf))
-
-    @pl.loop(0, depth // step, unroll=2)
-    def _(i):
-        at = pl.ds(pl.multiple_of(i * step, step), step)
-        turns = kv_raw[at].reshape(2 * step, kv_raw.shape[2])
-        for k in range(2):
-            kv[k, at, :] = dot32(picks[k], turns).astype(bf)
-
-    load(kv.at[0, :, head_cols(me_s)], wqk.at[block_of(me_s), pl.ds(own, own)], qk_r.at[me_s])
-    for k, head in enumerate((partner, me_s)):
-        load(kv.at[1, :, head_cols(head)], wv.at[block_of(in_half), pl.ds(k * own, own)],
-             v_r.at[in_half])
     pl.semaphore_wait(barrier, len(peers))
-    in_wout = load(coarse_out, wout, load_sem.at[6])
-    in_wup = load(up_weight, wup, load_sem.at[7])
-
     sent = []
     halo = remote(tokens, both.at[pl.ds(0, rows)], halo_s, halo_r, linear(after))
 
@@ -366,9 +341,9 @@
         sent.extend(later[r] + [direct[r, tp_bits[0]]])
 
     plan = PLAN
-    if sum(len(stage) for stage in PLAN) != seq - 1 + half - 1 + pieces:
+    if sum(len(stage) for stage in PLAN) != seq - 1 + half - 1 + pieces - 1:
         plan = [[("qk", d) for d in range(1, seq)] + [("v", d) for d in range(1, half)]]
-        plan[0] += [("down", r) for r in range(pieces)]
+        plan[0] += [("down", r) for r in range(1, pieces)]
 
     def issue(stage):
         for kind, d in plan[stage] if stage < len(plan) else ():
@@ -379,6 +354,31 @@
             else:
                 launch_down(d)
 
+    launch_down(0)
+    in_kv.wait()
+    in_wq = load(fine_query, wq, load_sem.at[2])
+    in_wkv = load(fine_keyval, wkv, load_sem.at[1])
+    in_wo = load(fine_out, wo, load_sem.at[3])
+    step = HEAD
+    picks = []
+    for k in range(2):
+        r = lax.broadcasted_iota(jnp.int32, (step, 2 * step), 0)
+        c = lax.broadcasted_iota(jnp.int32, (step, 2 * step), 1)
+        picks.append((c == 2 * r + k).astype(bf))
+
+    @pl.loop(0, depth // step, unroll=2)
+    def _(i):
+        at = pl.ds(pl.multiple_of(i * step, step), step)
+        turns = kv_raw[at].reshape(2 * step, kv_raw.shape[2])
+        for k in range(2):
+            kv[k, at, :] = dot32(picks[k], turns).astype(bf)
+
+    load(kv.at[0, :, head_cols(me_s)], wqk.at[block_of(me_s), pl.ds(own, own)], qk_r.at[me_s])
+    for k, head in enumerate((partner, me_s)):
+        load(kv.at[1, :, head_cols(head)], wv.at[block_of(in_half), pl.ds(k * own, own)],
+             v_r.at[in_half])
+    in_wout = load(coarse_out, wout, load_sem.at[6])
+    in_wup = load(up_weight, wup, load_sem.at[7])
     issue(0)
 
     in_fgain.wait()

time: 99.3 us -> 98.7 us (level)
  Pallas kernels: 97.8 us -> 96.7 us
    pallas_call x1, Pallas kernels: 97.8 us -> 96.7 us  [head_body(): pl.pallas_call(functools.partial(section_kernel, seq, tp), out_shape=jax....]
where the time goes in v8:
time: 98.7 us; the launch traced here: 97.6 us
  Pallas kernels  96.7 us (98%)
    pallas_call x1, Pallas kernels, head_body(): pl.pallas_call(functools.partial(section_kernel, seq, tp), out_shape=jax....  96.7 us

profile of v8, /device:TPU:19, one launch (start us, length us, event | category | flops | bytes accessed | tf_op | source)
XLA Modules:
  0.0 97.6 jit_solution(10594055214471827997)
XLA Ops:
  0.0 96.7 %shard_map.109 = bf16[256,1024]{1,0:T(8,128)(2,1)S(1)} custom-call(bf16[256,1024]{1,0:T(8,128)(2,1)} %tokens.1, f32[1,1024]{1,0:T(1,128)} %bitcast.3, bf16[1024,1024]{1,0:T(8,128)(2,1)} %fine_query.1, bf16[1024,2048]{1,0:T(8,128)(2,1)} %fine_keyval.1, bf16[1024,1024]{1,0:T(8,128)(2,1)} %fine_out.1, bf16[1024,1024]{1,0:T(8,128)(2,1)} %down_weight.1, ...), custom_call_target="tpu_custom_call" | custom-call | tf_op jit(solution)/shard_map/pallas_call | solution.py:788
  96.8 0.8 copy.13

commit v9 on v8

--- a/solution.py
+++ b/solution.py
@@ -177,8 +177,8 @@
 
 
 PLAN = (
-    (("qk", 4),),
-    (("v", 3), ("v", 1), ("v", 2), ("qk", 6), ("qk", 1)),
+    (("v", 3),),
+    (("v", 1), ("v", 2), ("qk", 6), ("qk", 1)),
     (),
     (("down", 1),),
     (("qk", 7),),
@@ -275,10 +275,11 @@
     sent = []
     halo = remote(tokens, both.at[pl.ds(0, rows)], halo_s, halo_r, linear(after))
 
-    def send_qk(offsets):
+    def send_qk(offsets, parts=(0, 1)):
         for n in offsets:
             dest = toggle(me_s, n)
-            for k, source in enumerate((coarse_query, kv.at[0])):
+            for k in parts:
+                source = (coarse_query, kv.at[0])[k]
                 sent.append(
                     remote(
                         source.at[:, head_cols(dest)], wqk.at[block_of(me_s), pl.ds(k * own, own)],
@@ -341,8 +342,8 @@
         sent.extend(later[r] + [direct[r, tp_bits[0]]])
 
     plan = PLAN
-    if sum(len(stage) for stage in PLAN) != seq - 1 + half - 1 + pieces - 1:
-        plan = [[("qk", d) for d in range(1, seq)] + [("v", d) for d in range(1, half)]]
+    if sum(len(stage) for stage in PLAN) != seq - 2 + half - 1 + pieces - 1:
+        plan = [[("qk", d) for d in range(1, seq) if d != half] + [("v", d) for d in range(1, half)]]
         plan[0] += [("down", r) for r in range(1, pieces)]
 
     def issue(stage):
@@ -355,6 +356,7 @@
                 launch_down(d)
 
     launch_down(0)
+    send_qk([half], (0,))
     in_kv.wait()
     in_wq = load(fine_query, wq, load_sem.at[2])
     in_wkv = load(fine_keyval, wkv, load_sem.at[1])
@@ -379,6 +381,7 @@
              v_r.at[in_half])
     in_wout = load(coarse_out, wout, load_sem.at[6])
     in_wup = load(up_weight, wup, load_sem.at[7])
+    send_qk([half], (1,))
     issue(0)
 
     in_fgain.wait()

time: 98.7 us -> 98.6 us (level)
  no operation moved by 1% of the time
where the time goes in v9:
time: 98.6 us; the launch traced here: 97.6 us
  Pallas kernels  96.8 us (98%)
    pallas_call x1, Pallas kernels, head_body(): pl.pallas_call(functools.partial(section_kernel, seq, tp), out_shape=jax....  96.8 us

profile of v9, /device:TPU:19, one launch (start us, length us, event | category | flops | bytes accessed | tf_op | source)
XLA Modules:
  0.0 97.6 jit_solution(17142947711105940415)
XLA Ops:
  0.0 96.8 %shard_map.109 = bf16[256,1024]{1,0:T(8,128)(2,1)S(1)} custom-call(bf16[256,1024]{1,0:T(8,128)(2,1)} %tokens.1, f32[1,1024]{1,0:T(1,128)} %bitcast.3, bf16[1024,1024]{1,0:T(8,128)(2,1)} %fine_query.1, bf16[1024,2048]{1,0:T(8,128)(2,1)} %fine_keyval.1, bf16[1024,1024]{1,0:T(8,128)(2,1)} %fine_out.1, bf16[1024,1024]{1,0:T(8,128)(2,1)} %down_weight.1, ...), custom_call_target="tpu_custom_call" | custom-call | tf_op jit(solution)/shard_map/pallas_call | solution.py:791
  96.8 0.8 copy.13
